TPU v7x, 32 devices: a whole 2x2x4 slice. The times are simulated.
32 devices in a mesh: seq: 8 (over z, x), tp: 4 (over y, core).
Axes of the slice: x: 2, y: 2, z: 4, core: 2. Of those that a mesh axis runs over, the one named last changes fastest.
Arguments:
- queries: bfloat16 [1536, 6144], P('seq', 'tp'), may hold values from -400 to 400
- key_vectors: bfloat16 [1536, 1024], P('seq', 'tp'), may hold values from -8 to 8
- value_vectors: bfloat16 [1536, 1024], P('seq', 'tp'), may hold values from -6 to 6
- positions: int32 [1536], P('seq'), may hold values from 0 to 1535, as said below
- residual: bfloat16 [1536, 6144], P('seq', 'tp'), may hold values from -200 to 200
- norm_gain: float32 [1, 6144], P(None, 'tp'), may hold values from 0.5 to 1.5
- out_weight: bfloat16 [6144, 6144], P('tp'), may hold values from -0.3125 to 0.3125
Outputs:
- quantized: bfloat16 [1536, 6144], P('seq')
- token_scale: float32 [1536], P('seq')
- new_residual: bfloat16 [1536, 6144], P('seq', 'tp')
Inputs may be any that keep to these rules, and one draw needn't show every extreme that they name: The positions are a permutation of 0 to 1535. Cut into 16 runs of 96 consecutive positions, the rows of one index of seq hold run r in their first 96 rows and run 2 * 8 - 1 - r in their last ones, both in increasing order, with r differing between the indices of seq.
All inputs are finite; a program needn't handle non-finite values. Where the computation divides by a largest or mean magnitude, that divisor is 1e-20 or more.
Results may differ from a plain program's by a relative error of at most 0.012.
Values may be sent and summed in bfloat16 or wider, within the bound.
A program may use at most 64 MiB of HBM per device.

v0:
```python
import functools
import math

import jax
import jax.numpy as jnp
from jax import lax
from jax.experimental import pallas as pl
from jax.experimental.pallas import tpu as pltpu
from jax.sharding import PartitionSpec as P

HEAD = 128
LOG2E = 1.4426950408889634
MASKED = -1e30
MESH = pl.DeviceIdType.MESH
F32 = jnp.float32
BF16 = jnp.bfloat16


def kernel(
    dims,
    pos_ref, key_ref, value_ref, gain_ref, query_hbm, residual_hbm, weight_hbm,
    quant_hbm, scale_hbm, stream_hbm,
    kv, pos_all, gain_all, query_raw, residual_raw, query, residual, weight,
    attended, part, from_core, pair, gained, quant, stream, scale,
    load_sem, kv_send, kv_recv, forward_send, pos_send, pos_recv, gain_send, gain_recv,
    core_send, core_recv, y_send, y_recv, out_send, out_recv, out_local,
):
    n_seq, n_tp, group, kv_count, half, tile = dims
    n_y = n_tp // 2
    me = lax.axis_index("seq")
    tp = lax.axis_index("tp")
    core = lax.rem(tp, 2)
    y = tp // 2
    core_peer = tp + 1 - 2 * core
    partner = me + 1 - 2 * lax.rem(me, 2)
    model = weight.shape[1]
    tiles = model // tile
    slice_width = model // n_tp
    tiles_slice = slice_width // tile
    own = half // 2
    keys = n_seq * half

    loads = [
        pltpu.make_async_copy(query_hbm, query_raw, load_sem.at[0]),
        pltpu.make_async_copy(residual_hbm, residual_raw, load_sem.at[1]),
        pltpu.make_async_copy(weight_hbm, weight, load_sem.at[2]),
    ]
    for load in loads:
        load.start()

    barrier = pltpu.get_barrier_semaphore()
    for step in range(1, n_seq):
        pl.semaphore_signal(
            barrier, inc=1, device_id=(lax.rem(me + step, n_seq), tp), device_id_type=MESH
        )
    for step in range(1, n_tp):
        pl.semaphore_signal(
            barrier, inc=1, device_id=(me, lax.rem(tp + step, n_tp)), device_id_type=MESH
        )

    first = pos_ref[0:1, 0:1].astype(F32)
    second = pos_ref[0:1, half : half + 1].astype(F32)
    keep = jnp.where(first < second, 1.0, 0.0)

    def split(ref):
        top = ref[:half, :].astype(F32)
        bottom = ref[half:, :].astype(F32)
        low = top * keep + bottom * (1.0 - keep)
        high = bottom * keep + top * (1.0 - keep)
        return low.astype(BF16), high.astype(BF16)

    for index, ref in enumerate((key_ref, value_ref)):
        low, high = split(ref)
        kv[0, me, index] = low
        kv[1, me, index] = high
    pos_all[me] = pos_ref[...]
    gain_all[tp] = gain_ref[...]
    pl.semaphore_wait(barrier, n_seq + n_tp - 2)

    line = n_seq // 2
    order = []
    for step in range(1, line // 2 + 1):
        order.append(step)
        if line - step != step:
            order.append(line - step)
    sent = []

    def remote(src, dst, send, recv, device):
        copy = pltpu.make_async_remote_copy(
            src_ref=src, dst_ref=dst, send_sem=send, recv_sem=recv,
            device_id=device, device_id_type=MESH,
        )
        copy.start()
        sent.append(copy)
        return copy

    def landed(dst, recv):
        pltpu.make_async_remote_copy(
            src_ref=dst, dst_ref=dst, send_sem=recv, recv_sem=recv,
            device_id=(partner, tp), device_id_type=MESH,
        ).wait_recv()

    def send_line(phase):
        for step in order:
            target = lax.rem(me + 2 * step, n_seq)
            remote(
                kv.at[phase, me], kv.at[phase, me], kv_send.at[phase, step],
                kv_recv.at[phase, me], (target, tp),
            )

    def send_partner(phase):
        remote(
            kv.at[phase, me], kv.at[phase, me], kv_send.at[phase, 0],
            kv_recv.at[phase, me], (partner, tp),
        )

    def forward(phase, step):
        source = lax.rem(me + 2 * step, n_seq)
        landed(kv.at[phase, source], kv_recv.at[phase, source])
        remote(
            kv.at[phase, source], kv.at[phase, source], forward_send.at[phase, step],
            kv_recv.at[phase, source], (partner, tp),
        )

    def arrivals(phase):
        for step in range(line):
            source = lax.rem(partner + 2 * step, n_seq)
            landed(kv.at[phase, source], kv_recv.at[phase, source])

    send_partner(0)
    send_line(0)
    for step in range(1, n_seq):
        remote(
            pos_ref, pos_all.at[me], pos_send.at[step], pos_recv.at[me],
            (lax.rem(me + step, n_seq), tp),
        )
    for step in range(1, n_tp):
        remote(
            gain_ref, gain_all.at[tp], gain_send.at[step], gain_recv.at[tp],
            (me, lax.rem(tp + step, n_tp)),
        )
    loads[0].wait()
    loads[1].wait()
    query[0], query[1] = split(query_raw)
    residual[0], residual[1] = split(residual_raw)
    for step in order:
        forward(0, step)
    send_line(1)
    send_partner(1)
    for step in range(1, n_seq):
        source = lax.rem(me + step, n_seq)
        landed(pos_all.at[source], pos_recv.at[source])
    arrivals(0)

    lanes = lax.broadcasted_iota(jnp.int32, (1, keys), 1)
    rows = lax.broadcasted_iota(jnp.int32, (half, 1), 0).astype(F32)

    def bias(phase):
        pick = jnp.minimum if phase == 0 else jnp.maximum

        def base(index):
            value = pos_all[index]
            return pick(value[0:1, 0:1].astype(F32), value[0:1, half : half + 1].astype(F32))

        key_pos = jnp.zeros((1, keys), F32)
        for source in range(n_seq):
            inside = (lanes >= source * half) & (lanes < (source + 1) * half)
            key_pos = jnp.where(
                inside, base(source) + (lanes - source * half).astype(F32), key_pos
            )
        return jnp.where(key_pos <= base(me) + rows, 0.0, MASKED)

    stack = group if keys <= 1024 else 1

    def attend(phase):
        mask = bias(phase)
        for head in range(0, kv_count * group, stack):
            kv_head = head // group
            columns = slice(kv_head * HEAD, (kv_head + 1) * HEAD)
            block = jnp.concatenate(
                [
                    query[phase, :, (head + i) * HEAD : (head + i + 1) * HEAD]
                    for i in range(stack)
                ],
                axis=0,
            )
            scores = []
            for piece in range(phase + 1):
                key_rows = kv[piece, :, 0, :, columns].reshape(keys, HEAD)
                value = lax.dot_general(
                    block, key_rows, (((1,), (1,)), ((), ())), preferred_element_type=F32
                ).reshape(stack, half, keys)
                scores.append(value + mask[None] if piece == phase else value)
            peak = jnp.max(scores[0], axis=2, keepdims=True)
            for value in scores[1:]:
                peak = jnp.maximum(peak, jnp.max(value, axis=2, keepdims=True))
            mixed = jnp.zeros((stack * half, HEAD), F32)
            total = jnp.zeros((stack, half, 1), F32)
            for piece, value in enumerate(scores):
                weights = jnp.exp2((value - peak) * (LOG2E / math.sqrt(HEAD)))
                total += jnp.sum(weights, axis=2, keepdims=True)
                value_rows = kv[piece, :, 1, :, columns].reshape(keys, HEAD)
                mixed += jnp.dot(
                    weights.astype(BF16).reshape(stack * half, keys), value_rows,
                    preferred_element_type=F32,
                )
            mixed = (mixed.reshape(stack, half, HEAD) / total).astype(BF16)
            for i in range(stack):
                attended[phase, :, (head + i) * HEAD : (head + i + 1) * HEAD] = mixed[i]

    def reduce_tile(phase, index):
        landed(from_core.at[phase, index], core_recv.at[phase, index])
        both = part[phase, index, core].astype(F32) + from_core[phase, index].astype(F32)
        pair[phase, y, index] = both.astype(BF16)
        for step in range(1, n_y):
            target = lax.rem(y + step, n_y) * 2 + core
            remote(
                pair.at[phase, y, index], pair.at[phase, y, index],
                y_send.at[phase, index, step], y_recv.at[phase, y, index], (me, target),
            )

    def project(phase, between):
        for index in range(tiles):
            columns = slice(index * tile, (index + 1) * tile)
            product = jnp.dot(
                attended[phase], weight[:, columns], preferred_element_type=F32
            )
            inner = (index % tiles_slice) * tile
            mine = jnp.where(tp == index // tiles_slice, 1.0, 0.0)
            product += residual[phase, :, inner : inner + tile].astype(F32) * mine
            part[phase, index] = product.astype(BF16).reshape(2, own, tile)
            remote(
                part.at[phase, index, 1 - core], from_core.at[phase, index],
                core_send.at[phase, index], core_recv.at[phase, index], (me, core_peer),
            )
            if index >= 1:
                reduce_tile(phase, index - 1)
            if index < len(between):
                between[index]()
        reduce_tile(phase, tiles - 1)
        for task in between[tiles:]:
            task()

    locals_out = []

    def finish(phase):
        square = jnp.zeros((own, 1), F32)
        peak = jnp.zeros((own, 1), F32)
        for index in range(tiles):
            for step in range(1, n_y):
                source = lax.rem(y + step, n_y)
                landed(pair.at[phase, source, index], y_recv.at[phase, source, index])
            total = pair[phase, 0, index].astype(F32)
            for source in range(1, n_y):
                total += pair[phase, source, index].astype(F32)
            inner = (index % tiles_slice) * tile
            stream[phase, index // tiles_slice, :, inner : inner + tile] = total.astype(BF16)
            square += jnp.sum(total * total, axis=1, keepdims=True)
            scaled = total * gain_all[index // tiles_slice, :, inner : inner + tile]
            gained[index] = scaled
            peak = jnp.maximum(peak, jnp.max(jnp.abs(scaled), axis=1, keepdims=True))
        inverse = lax.rsqrt(square / model + 1e-5)
        token = inverse * peak + 1e-6
        factor = inverse / token
        scale[phase] = jnp.broadcast_to(token, (own, 128))
        for index in range(tiles):
            quant[phase, :, index * tile : (index + 1) * tile] = (gained[index] * factor).astype(
                BF16
            )
        sends = (
            (quant.at[phase], quant.at[phase], quant_hbm),
            (stream.at[phase, tp], stream.at[phase, core_peer], stream_hbm),
            (scale.at[phase], scale.at[phase], scale_hbm),
        )
        for index, (here, there, out) in enumerate(sends):
            remote(
                there, out.at[phase, core], out_send.at[phase, index],
                out_recv.at[phase, index], (me, core_peer),
            )
            copy = pltpu.make_async_copy(here, out.at[phase, core], out_local.at[phase, index])
            copy.start()
            locals_out.append(copy)

    attend(0)
    loads[2].wait()
    project(0, [functools.partial(forward, 1, step) for step in order])
    arrivals(1)
    attend(1)
    project(1, [])
    for step in range(1, n_tp):
        source = lax.rem(tp + step, n_tp)
        landed(gain_all.at[source], gain_recv.at[source])
    finish(0)
    finish(1)
    for phase in range(2):
        for index, out in enumerate((quant_hbm, stream_hbm, scale_hbm)):
            landed(out.at[phase, 1 - core], out_recv.at[phase, index])
    for copy in locals_out:
        copy.wait()
    for copy in sent:
        copy.wait_send()


def on_device(n_seq, n_tp, queries, key_vectors, value_vectors, positions, residual, norm_gain, out_weight):
    token_rows, query_width = queries.shape
    half = token_rows // 2
    own = half // 2
    kv_width = key_vectors.shape[1]
    kv_count = kv_width // HEAD
    group = query_width // kv_width
    model = out_weight.shape[1]
    slice_width = residual.shape[1]
    tile = math.gcd(slice_width, 768)
    tiles = model // tile
    n_y = n_tp // 2
    vmem = pl.BlockSpec(memory_space=pltpu.VMEM)
    anywhere = pl.BlockSpec(memory_space=pl.ANY)
    dma = pltpu.SemaphoreType.DMA
    line = n_seq // 2
    quant, scale, stream = pl.pallas_call(
        functools.partial(kernel, (n_seq, n_tp, group, kv_count, half, tile)),
        out_shape=(
            jax.ShapeDtypeStruct((2, 2, own, model), BF16),
            jax.ShapeDtypeStruct((2, 2, own, 128), F32),
            jax.ShapeDtypeStruct((2, 2, own, slice_width), BF16),
        ),
        in_specs=[vmem, vmem, vmem, vmem, anywhere, anywhere, anywhere],
        out_specs=(anywhere, anywhere, anywhere),
        scratch_shapes=[
            pltpu.VMEM((2, n_seq, 2, half, kv_width), BF16),
            pltpu.VMEM((n_seq, 1, token_rows), jnp.int32),
            pltpu.VMEM((n_tp, 1, slice_width), F32),
            pltpu.VMEM(queries.shape, BF16),
            pltpu.VMEM(residual.shape, BF16),
            pltpu.VMEM((2, half, query_width), BF16),
            pltpu.VMEM((2, half, slice_width), BF16),
            pltpu.VMEM(out_weight.shape, BF16),
            pltpu.VMEM((2, half, query_width), BF16),
            pltpu.VMEM((2, tiles, 2, own, tile), BF16),
            pltpu.VMEM((2, tiles, own, tile), BF16),
            pltpu.VMEM((2, n_y, tiles, own, tile), BF16),
            pltpu.VMEM((tiles, own, tile), F32),
            pltpu.VMEM((2, own, model), BF16),
            pltpu.VMEM((2, n_tp, own, slice_width), BF16),
            pltpu.VMEM((2, own, 128), F32),
            dma((3,)),
            dma((2, line)),
            dma((2, n_seq)),
            dma((2, line)),
            dma((n_seq,)),
            dma((n_seq,)),
            dma((n_tp,)),
            dma((n_tp,)),
            dma((2, tiles)),
            dma((2, tiles)),
            dma((2, tiles, n_y)),
            dma((2, n_y, tiles)),
            dma((2, 3)),
            dma((2, 3)),
            dma((2, 3)),
        ],
        compiler_params=pltpu.CompilerParams(
            collective_id=0, has_side_effects=True, vmem_limit_bytes=63 * 1024 * 1024
        ),
    )(positions[None, :], key_vectors, value_vectors, norm_gain, queries, residual, out_weight)
    ordered = positions[0] < positions[half]

    def restore(value):
        top = jnp.where(ordered, value[0], value[1])
        bottom = jnp.where(ordered, value[1], value[0])
        return jnp.stack((top, bottom)).reshape((token_rows,) + value.shape[3:])

    return (restore(quant), restore(scale[..., 0]), restore(stream))


def solution(mesh):
    return jax.shard_map(
        functools.partial(on_device, mesh.shape["seq"], mesh.shape["tp"]),
        mesh=mesh,
        in_specs=(
            P("seq", "tp"),
            P("seq", "tp"),
            P("seq", "tp"),
            P("seq"),
            P("seq", "tp"),
            P(None, "tp"),
            P("tp", None),
        ),
        out_specs=(P("seq", None), P("seq"), P("seq", "tp")),
        check_vma=False,
    )
```

profile of v0, /device:TPU:0, one launch (start us, length us, event | category | flops | bytes accessed | tf_op | source)
XLA Modules:
  0.0 63.9 jit_solution(15224266114363438780)
XLA Ops:
  0.6 1.3 %fusion = (s32[1]{0:T(128)}, s32[1]{0:T(128)}) fusion(s32[192]{0:T(256)} %param.10), kind=kLoop, calls=%fused_computation.9 | loop fusion | bytes 16 | tf_op jit(solution)/shard_map/slice | solution.py:366
  3.3 55.6 %shard_map.94 = (bf16[2,2,48,6144]{3,2,1,0:T(8,128)(2,1)}, f32[2,2,48,128]{3,2,1,0:T(8,128)}, bf16[2,2,48,1536]{3,2,1,0:T(8,128)(2,1)}) custom-call(s32[1,192]{1,0:T(1,128)} %bitcast.8, bf16[192,256]{1,0:T(8,128)(2,1)} %key_ref.1, bf16[192,256]{1,0:T(8,128)(2,1)} %value_ref.1, f32[1,1536]{1,0:T(1,128)} %gain_ref.1, bf16[192,1536]{1,0:T(8,128)(2,1)} %query_hbm.1, ...), custom_call_target="tpu_custom_call" | custom-call | tf_op jit(solution)/shard_map/pallas_call | solution.py:320
  58.8 1.8 %broadcast_select_fusion.1 = (bf16[1,2,48,6144]{3,2,1,0:T(8,128)(2,1)S(1)}, bf16[1,2,48,6144]{3,2,1,0:T(8,128)(2,1)S(1)}) fusion(pred[]{:T(512)} %bitcast, bf16[2,2,48,6144]{3,2,1,0:T(8,128)(2,1)} %get-tuple-element.6), kind=kLoop, calls=%fused_computation.2 | loop fusion | flops 1179648 | bytes 4718593 | tf_op jit(solution)/shard_map/jit(_where)/select_n | solution.py:369
  60.6 0.0 copy-start.1
  60.6 0.0 copy-start
  60.6 1.6 %pad_maximum_fusion = bf16[2,2,48,6144]{3,2,1,0:T(8,128)(2,1)} fusion(bf16[1,2,48,6144]{3,2,1,0:T(8,128)(2,1)S(1)} %get-tuple-element.12, bf16[1,2,48,6144]{3,2,1,0:T(8,128)(2,1)S(1)} %get-tuple-element.11), kind=kLoop, calls=%fused_computation | loop fusion | flops 1179648 | bytes 4718592 | tf_op jit(solution)/shard_map/stack | solution.py:371
  62.2 0.0 copy-done.1
  62.2 0.1 select_reduce_fusion.1
  62.4 0.0 copy-done
  62.4 0.9 %pad_maximum_fusion.1 = bf16[2,2,48,1536]{3,2,1,0:T(8,128)(2,1)} fusion(bf16[1,2,48,1536]{3,2,1,0:T(8,128)(2,1)S(1)} %get-tuple-element.14, bf16[1,2,48,1536]{3,2,1,0:T(8,128)(2,1)S(1)} %get-tuple-element.13), kind=kLoop, calls=%fused_computation.3 | loop fusion | flops 294912 | bytes 1179648 | tf_op jit(solution)/shard_map/stack | solution.py:371
  63.3 0.6 %reshape.59 = f32[192]{0:T(256)} reshape(f32[2,2,48]{2,1,0:T(2,128)S(1)} %pad_maximum_fusion.2) | data formatting | bytes 1536 | tf_op jit(solution)/shard_map/reshape | solution.py:371
  (2 shorter events, 0.0 us)
Async XLA Ops:
  60.6 1.6 %copy-start.1 = (f32[2,2,48,128]{3,2,1,0:T(8,128)S(1)}, f32[2,2,48,128]{3,2,1,0:T(8,128)}, u32[]{:S(2)}) copy-start(f32[2,2,48,128]{3,2,1,0:T(8,128)} %get-tuple-element.7) | copy-start | bytes 294916
  60.6 1.7 %copy-start = (bf16[2,2,48,1536]{3,2,1,0:T(8,128)(2,1)S(1)}, bf16[2,2,48,1536]{3,2,1,0:T(8,128)(2,1)}, u32[]{:S(2)}) copy-start(bf16[2,2,48,1536]{3,2,1,0:T(8,128)(2,1)} %get-tuple-element.8) | copy-start | bytes 1769476
where the time goes:
time: 64.2 us; the launch traced here: 63.9 us
  Pallas kernels  55.6 us (87%)
  other arithmetic  4.41 us (7%)
  local copies, waits for them, and re-layouts  1.99 us (3%)
  between operations  1.98 us (3%)
    pallas_call x1, Pallas kernels, on_device(): pl.pallas_call(functools.partial(kernel, (n_seq, n_tp, group, kv_count, h...  55.6 us
    another operation x3, other arithmetic, restore(): return jnp.stack((top, bottom)).reshape((token_rows,) + value.shape[3:])  2.48 us
    select_n x3, other arithmetic, restore(): top = jnp.where(ordered, value[0], value[1])  1.93 us
    slice x1, local copies, waits for them, and re-layouts, on_device(): ordered = positions[0] < positions[half]  1.34 us

commit v1 on v0

--- a/solution.py
+++ b/solution.py
@@ -18,12 +18,12 @@
 
 def kernel(
     dims,
-    pos_ref, key_ref, value_ref, gain_ref, query_hbm, residual_hbm, weight_hbm,
-    quant_hbm, scale_hbm, stream_hbm,
-    kv, pos_all, gain_all, query_raw, residual_raw, query, residual, weight,
-    attended, part, from_core, pair, gained, quant, stream, scale,
+    pos_hbm, key_hbm, value_hbm, gain_hbm, query_hbm, residual_hbm, weight_hbm,
+    total_all, stat, gain_all, order_ref,
+    kv, pos_all, key_raw, value_raw, query_raw, residual_raw, query, residual, weight,
+    attended, part, from_core, pair,
     load_sem, kv_send, kv_recv, forward_send, pos_send, pos_recv, gain_send, gain_recv,
-    core_send, core_recv, y_send, y_recv, out_send, out_recv, out_local,
+    core_send, core_recv, y_send, y_recv, out_send, out_recv, stat_send, stat_recv,
 ):
     n_seq, n_tp, group, kv_count, half, tile = dims
     n_y = n_tp // 2
@@ -40,14 +40,6 @@
     own = half // 2
     keys = n_seq * half
 
-    loads = [
-        pltpu.make_async_copy(query_hbm, query_raw, load_sem.at[0]),
-        pltpu.make_async_copy(residual_hbm, residual_raw, load_sem.at[1]),
-        pltpu.make_async_copy(weight_hbm, weight, load_sem.at[2]),
-    ]
-    for load in loads:
-        load.start()
-
     barrier = pltpu.get_barrier_semaphore()
     for step in range(1, n_seq):
         pl.semaphore_signal(
@@ -58,9 +50,28 @@
             barrier, inc=1, device_id=(me, lax.rem(tp + step, n_tp)), device_id_type=MESH
         )
 
-    first = pos_ref[0:1, 0:1].astype(F32)
-    second = pos_ref[0:1, half : half + 1].astype(F32)
+    loads = [
+        pltpu.make_async_copy(source, target, load_sem.at[index])
+        for index, (source, target) in enumerate(
+            (
+                (pos_hbm, pos_all.at[me]),
+                (key_hbm, key_raw),
+                (value_hbm, value_raw),
+                (gain_hbm, gain_all.at[tp]),
+                (query_hbm, query_raw),
+                (residual_hbm, residual_raw),
+                (weight_hbm, weight),
+            )
+        )
+    ]
+    for load in loads:
+        load.start()
+    loads[0].wait()
+    own_pos = pos_all[me]
+    first = own_pos[0:1, 0:1].astype(F32)
+    second = own_pos[0:1, half : half + 1].astype(F32)
     keep = jnp.where(first < second, 1.0, 0.0)
+    order_ref[...] = jnp.broadcast_to(keep, order_ref.shape)
 
     def split(ref):
         top = ref[:half, :].astype(F32)
@@ -69,12 +80,12 @@
         high = bottom * keep + top * (1.0 - keep)
         return low.astype(BF16), high.astype(BF16)
 
-    for index, ref in enumerate((key_ref, value_ref)):
+    for index, ref in enumerate((key_raw, value_raw)):
+        loads[1 + index].wait()
         low, high = split(ref)
         kv[0, me, index] = low
         kv[1, me, index] = high
-    pos_all[me] = pos_ref[...]
-    gain_all[tp] = gain_ref[...]
+    loads[3].wait()
     pl.semaphore_wait(barrier, n_seq + n_tp - 2)
 
     line = n_seq // 2
@@ -131,16 +142,16 @@
     send_line(0)
     for step in range(1, n_seq):
         remote(
-            pos_ref, pos_all.at[me], pos_send.at[step], pos_recv.at[me],
+            pos_all.at[me], pos_all.at[me], pos_send.at[step], pos_recv.at[me],
             (lax.rem(me + step, n_seq), tp),
         )
     for step in range(1, n_tp):
         remote(
-            gain_ref, gain_all.at[tp], gain_send.at[step], gain_recv.at[tp],
+            gain_all.at[tp], gain_all.at[tp], gain_send.at[step], gain_recv.at[tp],
             (me, lax.rem(tp + step, n_tp)),
         )
-    loads[0].wait()
-    loads[1].wait()
+    loads[4].wait()
+    loads[5].wait()
     query[0], query[1] = split(query_raw)
     residual[0], residual[1] = split(residual_raw)
     for step in order:
@@ -241,8 +252,6 @@
         for task in between[tiles:]:
             task()
 
-    locals_out = []
-
     def finish(phase):
         square = jnp.zeros((own, 1), F32)
         peak = jnp.zeros((own, 1), F32)
@@ -254,35 +263,27 @@
             for source in range(1, n_y):
                 total += pair[phase, source, index].astype(F32)
             inner = (index % tiles_slice) * tile
-            stream[phase, index // tiles_slice, :, inner : inner + tile] = total.astype(BF16)
+            part_of = index // tiles_slice
+            total_all[phase, part_of, core, :, inner : inner + tile] = total.astype(BF16)
+            block = total_all.at[phase, part_of, core, :, inner : inner + tile]
+            remote(
+                block, block, out_send.at[phase, index], out_recv.at[phase, index],
+                (me, core_peer),
+            )
             square += jnp.sum(total * total, axis=1, keepdims=True)
-            scaled = total * gain_all[index // tiles_slice, :, inner : inner + tile]
-            gained[index] = scaled
+            scaled = total * gain_all[part_of, :, inner : inner + tile]
             peak = jnp.maximum(peak, jnp.max(jnp.abs(scaled), axis=1, keepdims=True))
         inverse = lax.rsqrt(square / model + 1e-5)
         token = inverse * peak + 1e-6
-        factor = inverse / token
-        scale[phase] = jnp.broadcast_to(token, (own, 128))
-        for index in range(tiles):
-            quant[phase, :, index * tile : (index + 1) * tile] = (gained[index] * factor).astype(
-                BF16
-            )
-        sends = (
-            (quant.at[phase], quant.at[phase], quant_hbm),
-            (stream.at[phase, tp], stream.at[phase, core_peer], stream_hbm),
-            (scale.at[phase], scale.at[phase], scale_hbm),
-        )
-        for index, (here, there, out) in enumerate(sends):
-            remote(
-                there, out.at[phase, core], out_send.at[phase, index],
-                out_recv.at[phase, index], (me, core_peer),
-            )
-            copy = pltpu.make_async_copy(here, out.at[phase, core], out_local.at[phase, index])
-            copy.start()
-            locals_out.append(copy)
+        stat[phase, core, 0] = jnp.broadcast_to(token, (own, 128))
+        stat[phase, core, 1] = jnp.broadcast_to(inverse / token, (own, 128))
+        remote(
+            stat.at[phase, core], stat.at[phase, core], stat_send.at[phase],
+            stat_recv.at[phase], (me, core_peer),
+        )
 
     attend(0)
-    loads[2].wait()
+    loads[6].wait()
     project(0, [functools.partial(forward, 1, step) for step in order])
     arrivals(1)
     attend(1)
@@ -293,12 +294,58 @@
     finish(0)
     finish(1)
     for phase in range(2):
-        for index, out in enumerate((quant_hbm, stream_hbm, scale_hbm)):
-            landed(out.at[phase, 1 - core], out_recv.at[phase, index])
-    for copy in locals_out:
-        copy.wait()
+        for index in range(tiles):
+            inner = (index % tiles_slice) * tile
+            landed(
+                total_all.at[phase, index // tiles_slice, 1 - core, :, inner : inner + tile],
+                out_recv.at[phase, index],
+            )
+        landed(stat.at[phase, 1 - core], stat_recv.at[phase])
     for copy in sent:
         copy.wait_send()
+
+
+def assemble(
+    dims, total_all, stat, gain_all, order_ref, quant_hbm, scale_ref, stream_hbm,
+    quant, stream, sem,
+):
+    n_tp, own, slice_width = dims
+    tp = lax.axis_index("tp")
+    swap = (jnp.max(order_ref[...]) < 0.5).astype(jnp.int32)
+    copies = []
+
+    def send(src, dst):
+        copy = pltpu.make_async_copy(src, dst, sem.at[len(copies)])
+        copy.start()
+        copies.append(copy)
+
+    scales = []
+    for top in range(2):
+        phase = swap if top == 0 else 1 - swap
+        for core in range(2):
+            rows = pl.ds((2 * top + core) * own, own)
+            stream[top, core] = total_all[phase, tp, core]
+            send(stream.at[top, core], stream_hbm.at[rows])
+            scales.append(stat[phase, core, 0])
+            factor = stat[phase, core, 1][:, 0:1]
+            for part in range(n_tp):
+                columns = slice(part * slice_width, (part + 1) * slice_width)
+                value = total_all[phase, part, core].astype(F32) * gain_all[part]
+                quant[top, core, :, columns] = (value * factor).astype(BF16)
+            send(quant.at[top, core], quant_hbm.at[rows])
+    scale = jnp.concatenate(scales, axis=0)
+    count = 4 * own
+    row = lax.broadcasted_iota(jnp.int32, (count, 128), 0)
+    lane = lax.broadcasted_iota(jnp.int32, (count, 128), 1)
+    pieces = [
+        jnp.sum(jnp.where(row == lane + start, scale, 0.0), axis=0, keepdims=True)
+        for start in range(0, count, 128)
+    ]
+    for index, piece in enumerate(pieces):
+        width = min(128, count - 128 * index)
+        scale_ref[:, 128 * index : 128 * index + width] = piece[:, :width]
+    for copy in copies:
+        copy.wait()
 
 
 def on_device(n_seq, n_tp, queries, key_vectors, value_vectors, positions, residual, norm_gain, out_weight):
@@ -317,19 +364,21 @@
     anywhere = pl.BlockSpec(memory_space=pl.ANY)
     dma = pltpu.SemaphoreType.DMA
     line = n_seq // 2
-    quant, scale, stream = pl.pallas_call(
+    middle = pl.pallas_call(
         functools.partial(kernel, (n_seq, n_tp, group, kv_count, half, tile)),
         out_shape=(
-            jax.ShapeDtypeStruct((2, 2, own, model), BF16),
-            jax.ShapeDtypeStruct((2, 2, own, 128), F32),
-            jax.ShapeDtypeStruct((2, 2, own, slice_width), BF16),
+            pltpu.VMEM((2, n_tp, 2, own, slice_width), BF16),
+            pltpu.VMEM((2, 2, 2, own, 128), F32),
+            pltpu.VMEM((n_tp, 1, slice_width), F32),
+            pltpu.VMEM((8, 128), F32),
         ),
-        in_specs=[vmem, vmem, vmem, vmem, anywhere, anywhere, anywhere],
-        out_specs=(anywhere, anywhere, anywhere),
+        in_specs=[anywhere] * 7,
+        out_specs=(vmem,) * 4,
         scratch_shapes=[
             pltpu.VMEM((2, n_seq, 2, half, kv_width), BF16),
             pltpu.VMEM((n_seq, 1, token_rows), jnp.int32),
-            pltpu.VMEM((n_tp, 1, slice_width), F32),
+            pltpu.VMEM(key_vectors.shape, BF16),
+            pltpu.VMEM(value_vectors.shape, BF16),
             pltpu.VMEM(queries.shape, BF16),
             pltpu.VMEM(residual.shape, BF16),
             pltpu.VMEM((2, half, query_width), BF16),
@@ -339,11 +388,7 @@
             pltpu.VMEM((2, tiles, 2, own, tile), BF16),
             pltpu.VMEM((2, tiles, own, tile), BF16),
             pltpu.VMEM((2, n_y, tiles, own, tile), BF16),
-            pltpu.VMEM((tiles, own, tile), F32),
-            pltpu.VMEM((2, own, model), BF16),
-            pltpu.VMEM((2, n_tp, own, slice_width), BF16),
-            pltpu.VMEM((2, own, 128), F32),
-            dma((3,)),
+            dma((7,)),
             dma((2, line)),
             dma((2, n_seq)),
             dma((2, line)),
@@ -355,22 +400,40 @@
             dma((2, tiles)),
             dma((2, tiles, n_y)),
             dma((2, n_y, tiles)),
-            dma((2, 3)),
-            dma((2, 3)),
-            dma((2, 3)),
+            dma((2, tiles)),
+            dma((2, tiles)),
+            dma((2,)),
+            dma((2,)),
         ],
         compiler_params=pltpu.CompilerParams(
-            collective_id=0, has_side_effects=True, vmem_limit_bytes=63 * 1024 * 1024
+            collective_id=0, has_side_effects=True, vmem_limit_bytes=48 * 1024 * 1024
         ),
-    )(positions[None, :], key_vectors, value_vectors, norm_gain, queries, residual, out_weight)
-    ordered = positions[0] < positions[half]
-
-    def restore(value):
-        top = jnp.where(ordered, value[0], value[1])
-        bottom = jnp.where(ordered, value[1], value[0])
-        return jnp.stack((top, bottom)).reshape((token_rows,) + value.shape[3:])
-
-    return (restore(quant), restore(scale[..., 0]), restore(stream))
+    )(
+        *(
+            pltpu.with_memory_space_constraint(value, pltpu.HBM)
+            for value in (
+                positions[None, :], key_vectors, value_vectors, norm_gain, queries, residual,
+                out_weight,
+            )
+        )
+    )
+    quant, scale, stream = pl.pallas_call(
+        functools.partial(assemble, (n_tp, own, slice_width)),
+        out_shape=(
+            jax.ShapeDtypeStruct((token_rows, model), BF16),
+            jax.ShapeDtypeStruct((1, token_rows), F32),
+            jax.ShapeDtypeStruct((token_rows, slice_width), BF16),
+        ),
+        in_specs=[vmem] * 4,
+        out_specs=(anywhere, vmem, anywhere),
+        scratch_shapes=[
+            pltpu.VMEM((2, 2, own, model), BF16),
+            pltpu.VMEM((2, 2, own, slice_width), BF16),
+            dma((8,)),
+        ],
+        compiler_params=pltpu.CompilerParams(vmem_limit_bytes=12 * 1024 * 1024),
+    )(*middle)
+    return (quant, scale.reshape(token_rows), stream)
 
 
 def solution(mesh):

time: 64.2 us -> 57.4 us (0.89); the launches traced: 63.9 us -> 56.5 us
  other arithmetic: 4.41 us -> 0 us
  local copies, waits for them, and re-layouts: 1.99 us -> 0 us
  between operations: 1.98 us -> 0.64 us
    pallas_call x0 -> x1, Pallas kernels: none -> 2.5 us  [on_device(): pl.pallas_call(functools.partial(assemble, (n_tp, own, slice_width)), out...]
    another operation x3 -> x0, other arithmetic: 2.48 us -> none  [restore(): return jnp.stack((top, bottom)).reshape((token_rows,) + value.shape[3:])]
    pallas_call x1, Pallas kernels: 55.6 us -> 53.4 us  [on_device(): pl.pallas_call(functools.partial(kernel, (n_seq, n_tp, group, kv_count, h...]
    select_n x3 -> x0, other arithmetic: 1.93 us -> none  [restore(): top = jnp.where(ordered, value[0], value[1])]
    slice x1 -> x0, local copies, waits for them, and re-layouts: 1.34 us -> none  [on_device(): ordered = positions[0] < positions[half]]
    reshape x1 -> x0, local copies, waits for them, and re-layouts: 0.65 us -> none  [restore(): return jnp.stack((top, bottom)).reshape((token_rows,) + value.shape[3:])]
where the time goes in v1:
time: 57.4 us; the launch traced here: 56.5 us
  Pallas kernels  55.9 us (97%)
  between operations  0.64 us (1%)
    pallas_call x1, Pallas kernels, on_device(): pl.pallas_call(functools.partial(kernel, (n_seq, n_tp, group, kv_count, h...  53.4 us
    pallas_call x1, Pallas kernels, on_device(): pl.pallas_call(functools.partial(assemble, (n_tp, own, slice_width)), out...  2.5 us

profile of v1, /device:TPU:0, one launch (start us, length us, event | category | flops | bytes accessed | tf_op | source)
XLA Modules:
  0.0 56.5 jit_solution(13113984132928708984)
XLA Ops:
  0.6 53.4 %shard_map.94 = (bf16[2,4,2,48,1536]{4,3,2,1,0:T(8,128)(2,1)S(1)}, f32[2,2,2,48,128]{4,3,2,1,0:T(8,128)S(1)}, f32[4,1,1536]{2,1,0:T(1,128)S(1)}, f32[8,128]{1,0:T(8,128)S(1)}) custom-call(s32[1,192]{1,0:T(1,128)} %bitcast.2, bf16[192,256]{1,0:T(8,128)(2,1)} %key_hbm.1, bf16[192,256]{1,0:T(8,128)(2,1)} %value_hbm.1, f32[1,1536]{1,0:T(1,128)} %gain_hbm.1, ...), custom_call_target="tpu_custom_call" | custom-call | tf_op jit(solution)/shard_map/pallas_call | solution.py:367
  54.0 2.5 %shard_map.95 = (bf16[192,6144]{1,0:T(8,128)(2,1)}, f32[1,192]{1,0:T(1,128)}, bf16[192,1536]{1,0:T(8,128)(2,1)}) custom-call(bf16[2,4,2,48,1536]{4,3,2,1,0:T(8,128)(2,1)S(1)} %get-tuple-element.10.total_all, f32[2,2,2,48,128]{4,3,2,1,0:T(8,128)S(1)} %get-tuple-element.11.stat, f32[4,1,1536]{2,1,0:T(1,128)S(1)} %get-tuple-element.12.gain_all, ...), custom_call_target="tpu_custom_call" | custom-call | tf_op jit(solution)/shard_map/pallas_call | solution.py:420

commit v2 on v1

--- a/solution.py
+++ b/solution.py
@@ -19,10 +19,10 @@
 def kernel(
     dims,
     pos_hbm, key_hbm, value_hbm, gain_hbm, query_hbm, residual_hbm, weight_hbm,
-    total_all, stat, gain_all, order_ref,
+    total_all, low_quant, stat, gain_all, order_ref,
     kv, pos_all, key_raw, value_raw, query_raw, residual_raw, query, residual, weight,
     attended, part, from_core, pair,
-    load_sem, kv_send, kv_recv, forward_send, pos_send, pos_recv, gain_send, gain_recv,
+    load_sem, x_send, x_recv, z_send, z_recv, pos_send, pos_recv, gain_send, gain_recv,
     core_send, core_recv, y_send, y_recv, out_send, out_recv, stat_send, stat_recv,
 ):
     n_seq, n_tp, group, kv_count, half, tile = dims
@@ -83,27 +83,26 @@
     for index, ref in enumerate((key_raw, value_raw)):
         loads[1 + index].wait()
         low, high = split(ref)
-        kv[0, me, index] = low
-        kv[1, me, index] = high
+        for head in range(kv_count):
+            columns = slice(head * HEAD, (head + 1) * HEAD)
+            kv[0, me, head, index] = low[:, columns]
+            kv[1, me, head, index] = high[:, columns]
     loads[3].wait()
     pl.semaphore_wait(barrier, n_seq + n_tp - 2)
 
     line = n_seq // 2
-    order = []
-    for step in range(1, line // 2 + 1):
-        order.append(step)
-        if line - step != step:
-            order.append(line - step)
-    sent = []
-
-    def remote(src, dst, send, recv, device):
+    row = me // 2
+    column = lax.rem(me, 2)
+
+    def remote(src, dst, send, recv, device, when=None):
         copy = pltpu.make_async_remote_copy(
             src_ref=src, dst_ref=dst, send_sem=send, recv_sem=recv,
             device_id=device, device_id_type=MESH,
         )
-        copy.start()
-        sent.append(copy)
-        return copy
+        if when is None:
+            copy.start()
+        else:
+            pl.when(when)(copy.start)
 
     def landed(dst, recv):
         pltpu.make_async_remote_copy(
@@ -111,57 +110,96 @@
             device_id=(partner, tp), device_id_type=MESH,
         ).wait_recv()
 
-    def send_line(phase):
-        for step in order:
-            target = lax.rem(me + 2 * step, n_seq)
-            remote(
-                kv.at[phase, me], kv.at[phase, me], kv_send.at[phase, step],
-                kv_recv.at[phase, me], (target, tp),
-            )
-
-    def send_partner(phase):
+    def left(src, send):
+        pltpu.make_async_remote_copy(
+            src_ref=src, dst_ref=src, send_sem=send, recv_sem=send,
+            device_id=(partner, tp), device_id_type=MESH,
+        ).wait_send()
+
+    def at_row(offset):
+        return lax.rem(me + 2 * offset + n_seq, n_seq)
+
+    def inside(offset):
+        return (row + offset >= 0) & (row + offset < line)
+
+    def along(phase, source, head, offset, when):
         remote(
-            kv.at[phase, me], kv.at[phase, me], kv_send.at[phase, 0],
-            kv_recv.at[phase, me], (partner, tp),
-        )
-
-    def forward(phase, step):
-        source = lax.rem(me + 2 * step, n_seq)
-        landed(kv.at[phase, source], kv_recv.at[phase, source])
+            kv.at[phase, source, head], kv.at[phase, source, head],
+            z_send.at[phase, head, 0 if offset > 0 else 1],
+            z_recv.at[phase, source // 2, head], (at_row(offset), tp), when,
+        )
+
+    def across(phase, source, head, when=None):
         remote(
-            kv.at[phase, source], kv.at[phase, source], forward_send.at[phase, step],
-            kv_recv.at[phase, source], (partner, tp),
-        )
+            kv.at[phase, source, head], kv.at[phase, source, head],
+            x_send.at[phase, head], x_recv.at[phase, head], (partner, tp), when,
+        )
+
+    def send_own(phase):
+        for head in range(kv_count):
+            across(phase, me, head)
+            for offset in (-1, 1, -3, 3):
+                if abs(offset) < line:
+                    along(phase, me, head, offset, inside(offset))
+
+    def relay(phase, distance):
+        for head in range(kv_count):
+            for side in (-1, 1):
+                source = at_row(side * distance)
+                there = inside(side * distance)
+
+                @pl.when(there)
+                def _():
+                    landed(kv.at[phase, source, head], z_recv.at[phase, source // 2, head])
+
+                if distance != 2:
+                    along(phase, source, head, -side, there & inside(-side))
+                if distance > 1:
+                    across(phase, source, head, there)
+            if distance == 1:
+                for side in (-1, 1):
+                    across(phase, at_row(side), head, inside(side))
+
+    distances = [d for d in (1, 3, 2) if d < line] + list(range(4, line))
 
     def arrivals(phase):
-        for step in range(line):
-            source = lax.rem(partner + 2 * step, n_seq)
-            landed(kv.at[phase, source], kv_recv.at[phase, source])
-
-    send_partner(0)
-    send_line(0)
+        for head in range(kv_count):
+            landed(kv.at[phase, 0:line, head], x_recv.at[phase, head])
+
+    def left_all(phase):
+        for head in range(kv_count):
+            left(kv.at[phase, 0:line, head], x_send.at[phase, head])
+            for index in range(line):
+                for slot, side in enumerate((1, -1)):
+                    room = line - 1 - index if side > 0 else index
+                    behind = line - 1 - room
+                    count = 0 if room < 1 else 1 + (room >= 3) + behind - (behind >= 2)
+                    if count:
+
+                        @pl.when(row == index)
+                        def _():
+                            left(kv.at[phase, 0:count, head], z_send.at[phase, head, slot])
+
+    send_own(0)
     for step in range(1, n_seq):
         remote(
-            pos_all.at[me], pos_all.at[me], pos_send.at[step], pos_recv.at[me],
+            pos_all.at[me], pos_all.at[me], pos_send.at[0], pos_recv.at[0],
             (lax.rem(me + step, n_seq), tp),
         )
     for step in range(1, n_tp):
         remote(
-            gain_all.at[tp], gain_all.at[tp], gain_send.at[step], gain_recv.at[tp],
+            gain_all.at[tp], gain_all.at[tp], gain_send.at[0], gain_recv.at[0],
             (me, lax.rem(tp + step, n_tp)),
         )
+    relay(0, distances[0])
     loads[4].wait()
     loads[5].wait()
     query[0], query[1] = split(query_raw)
     residual[0], residual[1] = split(residual_raw)
-    for step in order:
-        forward(0, step)
-    send_line(1)
-    send_partner(1)
-    for step in range(1, n_seq):
-        source = lax.rem(me + step, n_seq)
-        landed(pos_all.at[source], pos_recv.at[source])
-    arrivals(0)
+    for distance in distances[1:]:
+        relay(0, distance)
+    send_own(1)
+    landed(pos_all.at[0 : n_seq - 1], pos_recv.at[0])
 
     lanes = lax.broadcasted_iota(jnp.int32, (1, keys), 1)
     rows = lax.broadcasted_iota(jnp.int32, (half, 1), 0).astype(F32)
@@ -175,9 +213,9 @@
 
         key_pos = jnp.zeros((1, keys), F32)
         for source in range(n_seq):
-            inside = (lanes >= source * half) & (lanes < (source + 1) * half)
+            span = (lanes >= source * half) & (lanes < (source + 1) * half)
             key_pos = jnp.where(
-                inside, base(source) + (lanes - source * half).astype(F32), key_pos
+                span, base(source) + (lanes - source * half).astype(F32), key_pos
             )
         return jnp.where(key_pos <= base(me) + rows, 0.0, MASKED)
 
@@ -187,7 +225,6 @@
         mask = bias(phase)
         for head in range(0, kv_count * group, stack):
             kv_head = head // group
-            columns = slice(kv_head * HEAD, (kv_head + 1) * HEAD)
             block = jnp.concatenate(
                 [
                     query[phase, :, (head + i) * HEAD : (head + i + 1) * HEAD]
@@ -197,7 +234,7 @@
             )
             scores = []
             for piece in range(phase + 1):
-                key_rows = kv[piece, :, 0, :, columns].reshape(keys, HEAD)
+                key_rows = kv[piece, :, kv_head, 0].reshape(keys, HEAD)
                 value = lax.dot_general(
                     block, key_rows, (((1,), (1,)), ((), ())), preferred_element_type=F32
                 ).reshape(stack, half, keys)
@@ -210,7 +247,7 @@
             for piece, value in enumerate(scores):
                 weights = jnp.exp2((value - peak) * (LOG2E / math.sqrt(HEAD)))
                 total += jnp.sum(weights, axis=2, keepdims=True)
-                value_rows = kv[piece, :, 1, :, columns].reshape(keys, HEAD)
+                value_rows = kv[piece, :, kv_head, 1].reshape(keys, HEAD)
                 mixed += jnp.dot(
                     weights.astype(BF16).reshape(stack * half, keys), value_rows,
                     preferred_element_type=F32,
@@ -227,8 +264,10 @@
             target = lax.rem(y + step, n_y) * 2 + core
             remote(
                 pair.at[phase, y, index], pair.at[phase, y, index],
-                y_send.at[phase, index, step], y_recv.at[phase, y, index], (me, target),
-            )
+                y_send.at[phase, step - 1], y_recv.at[phase, n_y - 1 - step, index], (me, target),
+            )
+
+    lag = min(2, tiles)
 
     def project(phase, between):
         for index in range(tiles):
@@ -242,15 +281,15 @@
             part[phase, index] = product.astype(BF16).reshape(2, own, tile)
             remote(
                 part.at[phase, index, 1 - core], from_core.at[phase, index],
-                core_send.at[phase, index], core_recv.at[phase, index], (me, core_peer),
-            )
-            if index >= 1:
-                reduce_tile(phase, index - 1)
-            if index < len(between):
-                between[index]()
-        reduce_tile(phase, tiles - 1)
-        for task in between[tiles:]:
-            task()
+                core_send.at[phase], core_recv.at[phase, index], (me, core_peer),
+            )
+            if index >= lag:
+                reduce_tile(phase, index - lag)
+            for place, task in between:
+                if min(place, tiles - 1) == index:
+                    task()
+        for index in range(tiles - lag, tiles):
+            reduce_tile(phase, index)
 
     def finish(phase):
         square = jnp.zeros((own, 1), F32)
@@ -258,7 +297,7 @@
         for index in range(tiles):
             for step in range(1, n_y):
                 source = lax.rem(y + step, n_y)
-                landed(pair.at[phase, source, index], y_recv.at[phase, source, index])
+                landed(pair.at[phase, source, index], y_recv.at[phase, step - 1, index])
             total = pair[phase, 0, index].astype(F32)
             for source in range(1, n_y):
                 total += pair[phase, source, index].astype(F32)
@@ -267,7 +306,7 @@
             total_all[phase, part_of, core, :, inner : inner + tile] = total.astype(BF16)
             block = total_all.at[phase, part_of, core, :, inner : inner + tile]
             remote(
-                block, block, out_send.at[phase, index], out_recv.at[phase, index],
+                block, block, out_send.at[phase], out_recv.at[phase],
                 (me, core_peer),
             )
             square += jnp.sum(total * total, axis=1, keepdims=True)
@@ -282,32 +321,50 @@
             stat_recv.at[phase], (me, core_peer),
         )
 
+    def sends_left(phase):
+        left_all(phase)
+        left(part.at[phase, :, 1 - core], core_send.at[phase])
+        for step in range(1, n_y):
+            left(pair.at[phase, y], y_send.at[phase, step - 1])
+        left(total_all.at[phase, :, core], out_send.at[phase])
+        left(stat.at[phase, core], stat_send.at[phase])
+
+    def totals_landed(phase):
+        landed(total_all.at[phase, :, 1 - core], out_recv.at[phase])
+        landed(stat.at[phase, 1 - core], stat_recv.at[phase])
+
+    def normalize(phase):
+        for part_of in range(n_tp):
+            for owner in range(2):
+                value = total_all[phase, part_of, owner].astype(F32) * gain_all[part_of]
+                factor = stat[phase, owner, 1][:, 0:1]
+                columns = slice(part_of * slice_width, (part_of + 1) * slice_width)
+                low_quant[owner, :, columns] = (value * factor).astype(BF16)
+
+    arrivals(0)
     attend(0)
     loads[6].wait()
-    project(0, [functools.partial(forward, 1, step) for step in order])
+    project(
+        0, [(1 + 2 * i, functools.partial(relay, 1, d)) for i, d in enumerate(distances)]
+    )
     arrivals(1)
     attend(1)
     project(1, [])
-    for step in range(1, n_tp):
-        source = lax.rem(tp + step, n_tp)
-        landed(gain_all.at[source], gain_recv.at[source])
+    landed(gain_all.at[0 : n_tp - 1], gain_recv.at[0])
     finish(0)
+    totals_landed(0)
+    normalize(0)
+    sends_left(0)
+    left(pos_all.at[0 : n_seq - 1], pos_send.at[0])
+    left(gain_all.at[0 : n_tp - 1], gain_send.at[0])
     finish(1)
-    for phase in range(2):
-        for index in range(tiles):
-            inner = (index % tiles_slice) * tile
-            landed(
-                total_all.at[phase, index // tiles_slice, 1 - core, :, inner : inner + tile],
-                out_recv.at[phase, index],
-            )
-        landed(stat.at[phase, 1 - core], stat_recv.at[phase])
-    for copy in sent:
-        copy.wait_send()
+    totals_landed(1)
+    sends_left(1)
 
 
 def assemble(
-    dims, total_all, stat, gain_all, order_ref, quant_hbm, scale_ref, stream_hbm,
-    quant, stream, sem,
+    dims, total_all, low_quant, stat, gain_all, order_ref, quant_hbm, scale_hbm, stream_hbm,
+    quant, scale_row, sem,
 ):
     n_tp, own, slice_width = dims
     tp = lax.axis_index("tp")
@@ -319,31 +376,33 @@
         copy.start()
         copies.append(copy)
 
-    scales = []
-    for top in range(2):
-        phase = swap if top == 0 else 1 - swap
-        for core in range(2):
-            rows = pl.ds((2 * top + core) * own, own)
-            stream[top, core] = total_all[phase, tp, core]
-            send(stream.at[top, core], stream_hbm.at[rows])
-            scales.append(stat[phase, core, 0])
-            factor = stat[phase, core, 1][:, 0:1]
-            for part in range(n_tp):
-                columns = slice(part * slice_width, (part + 1) * slice_width)
-                value = total_all[phase, part, core].astype(F32) * gain_all[part]
-                quant[top, core, :, columns] = (value * factor).astype(BF16)
-            send(quant.at[top, core], quant_hbm.at[rows])
-    scale = jnp.concatenate(scales, axis=0)
+    def rows(phase, core):
+        place = swap if phase == 0 else 1 - swap
+        return pl.ds(pl.multiple_of((2 * place + core) * own, own), own)
+
+    for core in range(2):
+        send(low_quant.at[core], quant_hbm.at[rows(0, core)])
+        for phase in range(2):
+            send(total_all.at[phase, tp, core], stream_hbm.at[rows(phase, core)])
+    for core in range(2):
+        factor = stat[1, core, 1][:, 0:1]
+        for part in range(n_tp):
+            columns = slice(part * slice_width, (part + 1) * slice_width)
+            value = total_all[1, part, core].astype(F32) * gain_all[part]
+            quant[core, :, columns] = (value * factor).astype(BF16)
+            send(quant.at[core, :, columns], quant_hbm.at[rows(1, core), columns])
+    scale = jnp.concatenate(
+        [stat[swap if top == 0 else 1 - swap, core, 0] for top in range(2) for core in range(2)],
+        axis=0,
+    )
     count = 4 * own
     row = lax.broadcasted_iota(jnp.int32, (count, 128), 0)
     lane = lax.broadcasted_iota(jnp.int32, (count, 128), 1)
-    pieces = [
-        jnp.sum(jnp.where(row == lane + start, scale, 0.0), axis=0, keepdims=True)
-        for start in range(0, count, 128)
-    ]
-    for index, piece in enumerate(pieces):
-        width = min(128, count - 128 * index)
-        scale_ref[:, 128 * index : 128 * index + width] = piece[:, :width]
+    for start in range(0, count, 128):
+        piece = jnp.sum(jnp.where(row == lane + start, scale, 0.0), axis=0, keepdims=True)
+        width = min(128, count - start)
+        scale_row[:, start : start + width] = piece[:, :width]
+    send(scale_row, scale_hbm)
     for copy in copies:
         copy.wait()
 
@@ -357,7 +416,7 @@
     group = query_width // kv_width
     model = out_weight.shape[1]
     slice_width = residual.shape[1]
-    tile = math.gcd(slice_width, 768)
+    tile = math.gcd(slice_width, 512)
     tiles = model // tile
     n_y = n_tp // 2
     vmem = pl.BlockSpec(memory_space=pltpu.VMEM)
@@ -368,14 +427,15 @@
         functools.partial(kernel, (n_seq, n_tp, group, kv_count, half, tile)),
         out_shape=(
             pltpu.VMEM((2, n_tp, 2, own, slice_width), BF16),
+            pltpu.VMEM((2, own, model), BF16),
             pltpu.VMEM((2, 2, 2, own, 128), F32),
             pltpu.VMEM((n_tp, 1, slice_width), F32),
             pltpu.VMEM((8, 128), F32),
         ),
         in_specs=[anywhere] * 7,
-        out_specs=(vmem,) * 4,
+        out_specs=(vmem,) * 5,
         scratch_shapes=[
-            pltpu.VMEM((2, n_seq, 2, half, kv_width), BF16),
+            pltpu.VMEM((2, n_seq, kv_count, 2, half, HEAD), BF16),
             pltpu.VMEM((n_seq, 1, token_rows), jnp.int32),
             pltpu.VMEM(key_vectors.shape, BF16),
             pltpu.VMEM(value_vectors.shape, BF16),
@@ -389,19 +449,20 @@
             pltpu.VMEM((2, tiles, own, tile), BF16),
             pltpu.VMEM((2, n_y, tiles, own, tile), BF16),
             dma((7,)),
-            dma((2, line)),
-            dma((2, n_seq)),
-            dma((2, line)),
-            dma((n_seq,)),
-            dma((n_seq,)),
-            dma((n_tp,)),
-            dma((n_tp,)),
+            dma((2, kv_count)),
+            dma((2, kv_count)),
+            dma((2, kv_count, 2)),
+            dma((2, line, kv_count)),
+            dma((1,)),
+            dma((1,)),
+            dma((1,)),
+            dma((1,)),
+            dma((2,)),
             dma((2, tiles)),
-            dma((2, tiles)),
-            dma((2, tiles, n_y)),
-            dma((2, n_y, tiles)),
-            dma((2, tiles)),
-            dma((2, tiles)),
+            dma((2, n_y - 1)),
+            dma((2, n_y - 1, tiles)),
+            dma((2,)),
+            dma((2,)),
             dma((2,)),
             dma((2,)),
         ],
@@ -424,12 +485,12 @@
             jax.ShapeDtypeStruct((1, token_rows), F32),
             jax.ShapeDtypeStruct((token_rows, slice_width), BF16),
         ),
-        in_specs=[vmem] * 4,
-        out_specs=(anywhere, vmem, anywhere),
+        in_specs=[vmem] * 5,
+        out_specs=(anywhere,) * 3,
         scratch_shapes=[
-            pltpu.VMEM((2, 2, own, model), BF16),
-            pltpu.VMEM((2, 2, own, slice_width), BF16),
-            dma((8,)),
+            pltpu.VMEM((2, own, model), BF16),
+            pltpu.VMEM((1, token_rows), F32),
+            dma((7 + 2 * n_tp,)),
         ],
         compiler_params=pltpu.CompilerParams(vmem_limit_bytes=12 * 1024 * 1024),
     )(*middle)

time: 57.4 us -> 53.2 us (0.927); the launches traced: 56.5 us -> 53.1 us
  Pallas kernels: 55.9 us -> 52.4 us
    pallas_call x1, Pallas kernels: 53.4 us -> 50.6 us  [on_device(): pl.pallas_call(functools.partial(kernel, (n_seq, n_tp, group, kv_count, h...]
    pallas_call x1, Pallas kernels: 2.5 us -> 1.85 us  [on_device(): pl.pallas_call(functools.partial(assemble, (n_tp, own, slice_width)), out...]
where the time goes in v2:
time: 53.2 us; the launch traced here: 53.1 us
  Pallas kernels  52.4 us (98%)
  between operations  0.64 us (1%)
    pallas_call x1, Pallas kernels, on_device(): pl.pallas_call(functools.partial(kernel, (n_seq, n_tp, group, kv_count, h...  50.6 us
    pallas_call x1, Pallas kernels, on_device(): pl.pallas_call(functools.partial(assemble, (n_tp, own, slice_width)), out...  1.85 us

profile of v2, /device:TPU:0, one launch (start us, length us, event | category | flops | bytes accessed | tf_op | source)
XLA Modules:
  0.0 53.1 jit_solution(12873783135304318684)
XLA Ops:
  0.6 50.6 %shard_map.94 = (bf16[2,4,2,48,1536]{4,3,2,1,0:T(8,128)(2,1)S(1)}, bf16[2,48,6144]{2,1,0:T(8,128)(2,1)S(1)}, f32[2,2,2,48,128]{4,3,2,1,0:T(8,128)S(1)}, f32[4,1,1536]{2,1,0:T(1,128)S(1)}, f32[8,128]{1,0:T(8,128)S(1)}) custom-call(s32[1,192]{1,0:T(1,128)} %bitcast.2, bf16[192,256]{1,0:T(8,128)(2,1)} %key_hbm.1, bf16[192,256]{1,0:T(8,128)(2,1)} %value_hbm.1, ...), custom_call_target="tpu_custom_call" | custom-call | tf_op jit(solution)/shard_map/pallas_call | solution.py:426
  51.2 1.9 %shard_map.95 = (bf16[192,6144]{1,0:T(8,128)(2,1)}, f32[1,192]{1,0:T(1,128)}, bf16[192,1536]{1,0:T(8,128)(2,1)}) custom-call(bf16[2,4,2,48,1536]{4,3,2,1,0:T(8,128)(2,1)S(1)} %get-tuple-element.11.total_all, bf16[2,48,6144]{2,1,0:T(8,128)(2,1)S(1)} %get-tuple-element.12.low_quant, f32[2,2,2,48,128]{4,3,2,1,0:T(8,128)S(1)} %get-tuple-element.13.stat, ...), custom_call_target="tpu_custom_call" | custom-call | tf_op jit(solution)/shard_map/pallas_call | solution.py:481

commit v3 on v2

v3 whole, which is shorter than its diff:
```python
import functools
import math

import jax
import jax.numpy as jnp
from jax import lax
from jax.experimental import pallas as pl
from jax.experimental.pallas import tpu as pltpu
from jax.sharding import PartitionSpec as P

HEAD = 128
LOG2E = 1.4426950408889634
MASKED = -1e30
MESH = pl.DeviceIdType.MESH
F32 = jnp.float32
BF16 = jnp.bfloat16


def kernel(
    dims,
    pos_hbm, key_hbm, value_hbm, gain_hbm, query_hbm, residual_hbm, weight_hbm,
    total_all, low_quant, stat, gain_all, order_ref,
    kv, pos_own, key_raw, value_raw, query_raw, residual_raw, query, residual, weight,
    attended, part, from_core, pair,
    load_sem, x_send, x_recv, z_send, z_recv, gain_send, gain_recv,
    core_send, core_recv, y_send, y_recv, out_send, out_recv, stat_send, stat_recv,
):
    n_seq, n_tp, group, kv_count, half, tiles = dims
    n_y = n_tp // 2
    me = lax.axis_index("seq")
    tp = lax.axis_index("tp")
    core = lax.rem(tp, 2)
    y = tp // 2
    core_peer = tp + 1 - 2 * core
    partner = me + 1 - 2 * lax.rem(me, 2)
    model = weight.shape[1]
    slice_width = model // n_tp
    own = half // 2
    keys = n_seq * half
    line = n_seq // 2
    row = me // 2
    column = lax.rem(me, 2)

    def at_row(offset):
        return lax.rem(me + 2 * offset + n_seq, n_seq)

    def inside(offset):
        return (row + offset >= 0) & (row + offset < line)

    barrier = pltpu.get_barrier_semaphore()
    pl.semaphore_signal(barrier, inc=1, device_id=(partner, tp), device_id_type=MESH)
    greetings = n_tp
    for offset in (1, -1, 3):
        if abs(offset) < line:

            @pl.when(inside(offset))
            def _():
                pl.semaphore_signal(
                    barrier, inc=1, device_id=(at_row(offset), tp), device_id_type=MESH
                )

            greetings += jnp.where(inside(-offset), 1, 0)
    for step in range(1, n_tp):
        pl.semaphore_signal(
            barrier, inc=1, device_id=(me, lax.rem(tp + step, n_tp)), device_id_type=MESH
        )

    loads = [
        pltpu.make_async_copy(source, target, load_sem.at[index])
        for index, (source, target) in enumerate(
            (
                (pos_hbm, pos_own),
                (key_hbm, key_raw),
                (value_hbm, value_raw),
                (gain_hbm, gain_all.at[tp]),
                (query_hbm, query_raw),
                (residual_hbm, residual_raw),
                (weight_hbm, weight),
            )
        )
    ]
    for load in loads:
        load.start()
    loads[0].wait()
    first = pos_own[0:1, 0:1]
    second = pos_own[0:1, half : half + 1]
    keep = jnp.where(first < second, 1.0, 0.0)
    tile_row = lax.broadcasted_iota(jnp.int32, (16, HEAD), 0)
    start = jnp.where(tile_row < 2, jnp.minimum(first, second), jnp.maximum(first, second))
    digit = jnp.where((tile_row & 1) == 0, start >> 6, start & 63)
    kv[0, row, column, 0, 2 * half :] = digit.astype(F32).astype(BF16)
    order_ref[...] = jnp.broadcast_to(keep, order_ref.shape)

    def split(ref):
        top = ref[:half, :].astype(F32)
        bottom = ref[half:, :].astype(F32)
        low = top * keep + bottom * (1.0 - keep)
        high = bottom * keep + top * (1.0 - keep)
        return low.astype(BF16), high.astype(BF16)

    for index, ref in enumerate((key_raw, value_raw)):
        loads[1 + index].wait()
        low, high = split(ref)
        for head in range(kv_count):
            columns = slice(head * HEAD, (head + 1) * HEAD)
            kind = slice(index * half, (index + 1) * half)
            kv[0, row, column, head, kind] = low[:, columns]
            kv[1, row, column, head, kind] = high[:, columns]
    loads[3].wait()
    pl.semaphore_wait(barrier, greetings)


    def remote(src, dst, send, recv, device, when=None):
        copy = pltpu.make_async_remote_copy(
            src_ref=src, dst_ref=dst, send_sem=send, recv_sem=recv,
            device_id=device, device_id_type=MESH,
        )
        if when is None:
            copy.start()
        else:
            pl.when(when)(copy.start)

    def landed(dst, recv):
        pltpu.make_async_remote_copy(
            src_ref=dst, dst_ref=dst, send_sem=recv, recv_sem=recv,
            device_id=(partner, tp), device_id_type=MESH,
        ).wait_recv()

    def left(src, send):
        pltpu.make_async_remote_copy(
            src_ref=src, dst_ref=src, send_sem=send, recv_sem=send,
            device_id=(partner, tp), device_id_type=MESH,
        ).wait_send()

    def span(phase, head):
        return slice(0, 2 * half + 16 * (phase == 0 and head == 0))

    def block(phase, source, head):
        return kv.at[phase, source // 2, lax.rem(source, 2), head, span(phase, head)]

    def along(phase, source, head, offset, when):
        side = 0 if offset > 0 else 1
        target = (at_row(offset), tp)
        remote(
            block(phase, source, head), block(phase, source, head),
            z_send.at[phase, head, side], z_recv.at[phase, source // 2, head], target, when,
        )

    def across(phase, source, head, when=None):
        remote(
            block(phase, source, head), block(phase, source, head),
            x_send.at[phase, head], x_recv.at[phase, head], (partner, tp), when,
        )

    def send_own(phase):
        for head in range(kv_count):
            across(phase, me, head)
            for offset in (-1, -3, 1) if phase == 0 else (-1, 1, -3, 3):
                if abs(offset) < line:
                    along(phase, me, head, offset, inside(offset))

    def relay(phase, side, distance):
        source = at_row(side * distance)
        there = inside(side * distance)
        for head in range(kv_count):

            @pl.when(there)
            def _():
                landed(block(phase, source, head), z_recv.at[phase, source // 2, head])

            if distance != 2 or (phase == 0 and side < 0):
                along(phase, source, head, -side, there & inside(-side))
            across(phase, source, head, there)

    relays = [(-1, d) for d in range(1, line)]
    relays += [(1, d) for d in (1, 3, 2) if d < line] + [(1, d) for d in range(4, line)]

    def arrivals(phase):
        for head in range(kv_count):
            landed(kv.at[phase, :, 0, head, span(phase, head)], x_recv.at[phase, head])

    def left_all(phase):
        for head in range(kv_count):
            left(kv.at[phase, :, 0, head, span(phase, head)], x_send.at[phase, head])
        for index in range(line):
            ahead = line - 1 - index
            counts = (
                1 + (phase == 1 and ahead >= 3) + index - (phase == 1 and index >= 2)
                if ahead
                else 0,
                1 + (index >= 3) + ahead - (ahead >= 2) if index else 0,
            )

            @pl.when(row == index)
            def _():
                for side, count in enumerate(counts):
                    if count == 0:
                        continue
                    for head in range(kv_count):
                        left(
                            kv.at[phase, 0:count, 0, head, span(phase, head)],
                            z_send.at[phase, head, side],
                        )

    send_own(0)
    for step in range(1, n_tp):
        remote(
            gain_all.at[tp], gain_all.at[tp], gain_send.at[0], gain_recv.at[0],
            (me, lax.rem(tp + step, n_tp)),
        )
    loads[4].wait()
    loads[5].wait()
    query[0], query[1] = split(query_raw)
    residual[0], residual[1] = split(residual_raw)
    for side, distance in relays:
        relay(0, side, distance)
    send_own(1)

    rows = lax.broadcasted_iota(jnp.int32, (half, 1), 0).astype(F32)

    def bias(phase, sources):
        lanes = lax.broadcasted_iota(jnp.int32, (1, len(sources) * half), 1)

        def base(index):
            digits = kv[0, index // 2, lax.rem(index, 2), 0, 2 * half :].astype(F32)
            return digits[2 * phase : 2 * phase + 1, 0:1] * 64.0 + digits[
                2 * phase + 1 : 2 * phase + 2, 0:1
            ]

        key_pos = jnp.zeros(lanes.shape, F32)
        for index, source in enumerate(sources):
            within = (lanes >= index * half) & (lanes < (index + 1) * half)
            key_pos = jnp.where(within, base(source) + (lanes - index * half).astype(F32), key_pos)
        return jnp.where(key_pos <= base(me) + rows, 0.0, MASKED)

    stack = group if keys <= 1024 else 1
    heads = range(0, kv_count * group, stack)
    slope = LOG2E / math.sqrt(HEAD)

    def queries_of(phase, head):
        return jnp.concatenate(
            [query[phase, :, (head + i) * HEAD : (head + i + 1) * HEAD] for i in range(stack)],
            axis=0,
        )

    def scores_of(block_rows, key_rows, mask):
        count = key_rows.shape[0]
        value = lax.dot_general(
            block_rows, key_rows, (((1,), (1,)), ((), ())), preferred_element_type=F32
        ).reshape(stack, half, count)
        return value if mask is None else value + mask[None]

    def weigh(value, peak, value_rows):
        weights = jnp.exp2((value - peak) * slope)
        mixed = jnp.dot(
            weights.astype(BF16).reshape(stack * half, value.shape[2]), value_rows,
            preferred_element_type=F32,
        ).reshape(stack, half, HEAD)
        return jnp.sum(weights, axis=2, keepdims=True), mixed

    def put(phase, head, mixed):
        for i in range(stack):
            attended[phase, :, (head + i) * HEAD : (head + i + 1) * HEAD] = mixed[i].astype(BF16)

    def attend_column(side, before):
        place = column if side == 0 else 1 - column
        mask = bias(0, [2 * index + place for index in range(line)])
        results = []
        for index, head in enumerate(heads):
            key_rows, value_rows = (
                kv[0, :, place, head // group, kind * half : (kind + 1) * half].reshape(
                    line * half, HEAD
                )
                for kind in range(2)
            )
            value = scores_of(queries_of(0, head), key_rows, mask)
            peak = jnp.max(value, axis=2, keepdims=True)
            if side == 0:
                results.append((peak, *weigh(value, peak, value_rows)))
                continue
            old_peak, old_total, old_mixed = before[index]
            peak = jnp.maximum(peak, old_peak)
            total, mixed = weigh(value, peak, value_rows)
            shrink = jnp.exp2((old_peak - peak) * slope)
            put(0, head, (mixed + old_mixed * shrink) / (total + old_total * shrink))
        return results

    def attend(phase):
        mask = bias(phase, list(range(n_seq)))
        for head in heads:
            kv_head = head // group
            block_rows = queries_of(phase, head)
            scores = [
                scores_of(
                    block_rows, kv[piece, :, :, kv_head, :half].reshape(keys, HEAD),
                    mask if piece == phase else None,
                )
                for piece in range(phase + 1)
            ]
            peak = jnp.max(scores[0], axis=2, keepdims=True)
            for value in scores[1:]:
                peak = jnp.maximum(peak, jnp.max(value, axis=2, keepdims=True))
            mixed = jnp.zeros((stack, half, HEAD), F32)
            total = jnp.zeros((stack, half, 1), F32)
            for piece, value in enumerate(scores):
                more, added = weigh(
                    value, peak, kv[piece, :, :, kv_head, half : 2 * half].reshape(keys, HEAD)
                )
                total += more
                mixed += added
            put(phase, head, mixed / total)

    def reduce_tile(phase, index):
        columns = tiles[index][2]
        landed(from_core.at[phase, :, columns], core_recv.at[phase, index])
        both = part[phase, core, :, columns].astype(F32) + from_core[phase, :, columns].astype(F32)
        pair[phase, y, :, columns] = both.astype(BF16)
        for step in range(1, n_y):
            target = lax.rem(y + step, n_y) * 2 + core
            remote(
                pair.at[phase, y, :, columns], pair.at[phase, y, :, columns],
                y_send.at[phase, step - 1], y_recv.at[phase, n_y - 1 - step, index], (me, target),
            )

    def project(phase, between):
        done = 0
        for index, (part_of, inner, columns) in enumerate(tiles):
            product = jnp.dot(
                attended[phase], weight[:, columns], preferred_element_type=F32
            )
            mine = jnp.where(tp == part_of, 1.0, 0.0)
            product += residual[phase, :, inner].astype(F32) * mine
            part[phase, 0, :, columns] = product[:own].astype(BF16)
            part[phase, 1, :, columns] = product[own:].astype(BF16)
            remote(
                part.at[phase, 1 - core, :, columns], from_core.at[phase, :, columns],
                core_send.at[phase], core_recv.at[phase, index], (me, core_peer),
            )
            ready = 1 if index < 4 else 2
            while done + ready <= index:
                reduce_tile(phase, done)
                done += 1
            for place, task in between:
                if min(place, len(tiles) - 1) == index:
                    task()
        for index in range(done, len(tiles)):
            reduce_tile(phase, index)

    def finish(phase):
        square = jnp.zeros((own, 1), F32)
        peak = jnp.zeros((own, 1), F32)
        for index, (part_of, inner, columns) in enumerate(tiles):
            for step in range(1, n_y):
                source = lax.rem(y + step, n_y)
                landed(pair.at[phase, source, :, columns], y_recv.at[phase, step - 1, index])
            total = pair[phase, 0, :, columns].astype(F32)
            for source in range(1, n_y):
                total += pair[phase, source, :, columns].astype(F32)
            total_all[phase, part_of, core, :, inner] = total.astype(BF16)
            piece = total_all.at[phase, part_of, core, :, inner]
            remote(piece, piece, out_send.at[phase], out_recv.at[phase], (me, core_peer))
            square += jnp.sum(total * total, axis=1, keepdims=True)
            scaled = total * gain_all[part_of, :, inner]
            peak = jnp.maximum(peak, jnp.max(jnp.abs(scaled), axis=1, keepdims=True))
        inverse = lax.rsqrt(square / model + 1e-5)
        token = inverse * peak + 1e-6
        stat[phase, core, 0] = jnp.broadcast_to(token, (own, 128))
        stat[phase, core, 1] = jnp.broadcast_to(inverse / token, (own, 128))
        remote(
            stat.at[phase, core], stat.at[phase, core], stat_send.at[phase],
            stat_recv.at[phase], (me, core_peer),
        )

    def sends_left(phase):
        left_all(phase)
        left(part.at[phase, 1 - core], core_send.at[phase])
        for step in range(1, n_y):
            left(pair.at[phase, y], y_send.at[phase, step - 1])
        left(total_all.at[phase, :, core], out_send.at[phase])
        left(stat.at[phase, core], stat_send.at[phase])

    def totals_landed(phase):
        landed(total_all.at[phase, :, 1 - core], out_recv.at[phase])
        landed(stat.at[phase, 1 - core], stat_recv.at[phase])

    def normalize(phase):
        for part_of in range(n_tp):
            for owner in range(2):
                value = total_all[phase, part_of, owner].astype(F32) * gain_all[part_of]
                factor = stat[phase, owner, 1][:, 0:1]
                columns = slice(part_of * slice_width, (part_of + 1) * slice_width)
                low_quant[owner, :, columns] = (value * factor).astype(BF16)

    near = attend_column(0, None)
    arrivals(0)
    attend_column(1, near)
    loads[6].wait()
    later = [d for d in (1, 3, 2) if d < line] + list(range(4, line))
    project(
        0,
        [
            (1 + 2 * i, functools.partial(relay, 1, side, distance))
            for i, distance in enumerate(later)
            for side in (-1, 1)
        ],
    )
    arrivals(1)
    attend(1)
    project(1, [])
    landed(gain_all.at[0 : n_tp - 1], gain_recv.at[0])
    finish(0)
    totals_landed(0)
    normalize(0)
    sends_left(0)
    left(gain_all.at[0 : n_tp - 1], gain_send.at[0])
    finish(1)
    totals_landed(1)
    sends_left(1)


def assemble(
    dims, total_all, low_quant, stat, gain_all, order_ref, quant_hbm, scale_hbm, stream_hbm,
    quant, scale_row, sem,
):
    n_tp, own, slice_width = dims
    tp = lax.axis_index("tp")
    swap = (jnp.max(order_ref[...]) < 0.5).astype(jnp.int32)

    def send(src, dst, index):
        pltpu.make_async_copy(src, dst, sem.at[index]).start()

    def rows(phase, core):
        place = swap if phase == 0 else 1 - swap
        return pl.ds(pl.multiple_of((2 * place + core) * own, own), own)

    for core in range(2):
        send(low_quant.at[core], quant_hbm.at[rows(0, core)], 0)
        for phase in range(2):
            send(total_all.at[phase, tp, core], stream_hbm.at[rows(phase, core)], 1)
    for core in range(2):
        factor = stat[1, core, 1][:, 0:1]
        for part in range(n_tp):
            columns = slice(part * slice_width, (part + 1) * slice_width)
            value = total_all[1, part, core].astype(F32) * gain_all[part]
            quant[core, :, columns] = (value * factor).astype(BF16)
            send(quant.at[core, :, columns], quant_hbm.at[rows(1, core), columns], 0)
    scale = jnp.concatenate(
        [stat[swap if top == 0 else 1 - swap, core, 0] for top in range(2) for core in range(2)],
        axis=0,
    )
    count = 4 * own
    row = lax.broadcasted_iota(jnp.int32, (count, 128), 0)
    lane = lax.broadcasted_iota(jnp.int32, (count, 128), 1)
    for start in range(0, count, 128):
        piece = jnp.sum(jnp.where(row == lane + start, scale, 0.0), axis=0, keepdims=True)
        width = min(128, count - start)
        scale_row[:, start : start + width] = piece[:, :width]
    send(scale_row, scale_hbm, 2)
    for index, array in enumerate((quant_hbm, stream_hbm, scale_hbm)):
        pltpu.make_async_copy(array, array, sem.at[index]).wait()


def tiles_of(n_tp, slice_width):
    if slice_width % 768:
        widths = [[slice_width]] * n_tp
    else:
        first = [256, 512] + [768] * (slice_width // 768 - 1)
        widths = [first] + [[768] * (slice_width // 768)] * (n_tp - 2) + [first[::-1]]
    tiles = []
    for index, row in enumerate(widths):
        inner = 0
        for width in row:
            start = index * slice_width + inner
            tiles.append((index, slice(inner, inner + width), slice(start, start + width)))
            inner += width
    return tiles


def on_device(n_seq, n_tp, queries, key_vectors, value_vectors, positions, residual, norm_gain, out_weight):
    token_rows, query_width = queries.shape
    half = token_rows // 2
    own = half // 2
    kv_width = key_vectors.shape[1]
    kv_count = kv_width // HEAD
    group = query_width // kv_width
    model = out_weight.shape[1]
    slice_width = residual.shape[1]
    tiles = tiles_of(n_tp, slice_width)
    count = len(tiles)
    n_y = n_tp // 2
    vmem = pl.BlockSpec(memory_space=pltpu.VMEM)
    anywhere = pl.BlockSpec(memory_space=pl.ANY)
    dma = pltpu.SemaphoreType.DMA
    line = n_seq // 2
    middle = pl.pallas_call(
        functools.partial(kernel, (n_seq, n_tp, group, kv_count, half, tiles)),
        out_shape=(
            pltpu.VMEM((2, n_tp, 2, own, slice_width), BF16),
            pltpu.VMEM((2, own, model), BF16),
            pltpu.VMEM((2, 2, 2, own, 128), F32),
            pltpu.VMEM((n_tp, 1, slice_width), F32),
            pltpu.VMEM((8, 128), F32),
        ),
        in_specs=[anywhere] * 7,
        out_specs=(vmem,) * 5,
        scratch_shapes=[
            pltpu.VMEM((2, line, 2, kv_count, 2 * half + 16, HEAD), BF16),
            pltpu.VMEM((1, token_rows), jnp.int32),
            pltpu.VMEM(key_vectors.shape, BF16),
            pltpu.VMEM(value_vectors.shape, BF16),
            pltpu.VMEM(queries.shape, BF16),
            pltpu.VMEM(residual.shape, BF16),
            pltpu.VMEM((2, half, query_width), BF16),
            pltpu.VMEM((2, half, slice_width), BF16),
            pltpu.VMEM(out_weight.shape, BF16),
            pltpu.VMEM((2, half, query_width), BF16),
            pltpu.VMEM((2, 2, own, model), BF16),
            pltpu.VMEM((2, own, model), BF16),
            pltpu.VMEM((2, n_y, own, model), BF16),
            dma((7,)),
            dma((2, kv_count)),
            dma((2, kv_count)),
            dma((2, kv_count, 2)),
            dma((2, line, kv_count)),
            dma((1,)),
            dma((1,)),
            dma((2,)),
            dma((2, count)),
            dma((2, n_y - 1)),
            dma((2, n_y - 1, count)),
            dma((2,)),
            dma((2,)),
            dma((2,)),
            dma((2,)),
        ],
        compiler_params=pltpu.CompilerParams(
            collective_id=0, has_side_effects=True, vmem_limit_bytes=48 * 1024 * 1024
        ),
    )(
        *(
            pltpu.with_memory_space_constraint(value, pltpu.HBM)
            for value in (
                positions[None, :], key_vectors, value_vectors, norm_gain, queries, residual,
                out_weight,
            )
        )
    )
    quant, scale, stream = pl.pallas_call(
        functools.partial(assemble, (n_tp, own, slice_width)),
        out_shape=(
            jax.ShapeDtypeStruct((token_rows, model), BF16),
            jax.ShapeDtypeStruct((1, token_rows), F32),
            jax.ShapeDtypeStruct((token_rows, slice_width), BF16),
        ),
        in_specs=[vmem] * 5,
        out_specs=(anywhere,) * 3,
        scratch_shapes=[
            pltpu.VMEM((2, own, model), BF16),
            pltpu.VMEM((1, token_rows), F32),
            dma((3,)),
        ],
        compiler_params=pltpu.CompilerParams(vmem_limit_bytes=12 * 1024 * 1024),
    )(*middle)
    return (quant, scale.reshape(token_rows), stream)


def solution(mesh):
    return jax.shard_map(
        functools.partial(on_device, mesh.shape["seq"], mesh.shape["tp"]),
        mesh=mesh,
        in_specs=(
            P("seq", "tp"),
            P("seq", "tp"),
            P("seq", "tp"),
            P("seq"),
            P("seq", "tp"),
            P(None, "tp"),
            P("tp", None),
        ),
        out_specs=(P("seq", None), P("seq"), P("seq", "tp")),
        check_vma=False,
    )
```

time: 53.2 us -> 52.1 us (0.979)
  Pallas kernels: 52.4 us -> 51.3 us
    pallas_call x1, Pallas kernels: 50.6 us -> 49.5 us  [on_device(): pl.pallas_call(functools.partial(kernel, (n_seq, n_tp, group, kv_count, h...]
where the time goes in v3:
time: 52.1 us; the launch traced here: 51.9 us
  Pallas kernels  51.3 us (98%)
  between operations  0.64 us (1%)
    pallas_call x1, Pallas kernels, on_device(): pl.pallas_call(functools.partial(kernel, (n_seq, n_tp, group, kv_count, h...  49.5 us
    pallas_call x1, Pallas kernels, on_device(): pl.pallas_call(functools.partial(assemble, (n_tp, own, slice_width)), out...  1.75 us

profile of v3, /device:TPU:0, one launch (start us, length us, event | category | flops | bytes accessed | tf_op | source)
XLA Modules:
  0.0 51.9 jit_solution(12760025354018617150)
XLA Ops:
  0.6 49.5 %shard_map.94 = (bf16[2,4,2,48,1536]{4,3,2,1,0:T(8,128)(2,1)S(1)}, bf16[2,48,6144]{2,1,0:T(8,128)(2,1)S(1)}, f32[2,2,2,48,128]{4,3,2,1,0:T(8,128)S(1)}, f32[4,1,1536]{2,1,0:T(1,128)S(1)}, f32[8,128]{1,0:T(8,128)S(1)}) custom-call(s32[1,192]{1,0:T(1,128)} %bitcast.2, bf16[192,256]{1,0:T(8,128)(2,1)} %key_hbm.1, bf16[192,256]{1,0:T(8,128)(2,1)} %value_hbm.1, ...), custom_call_target="tpu_custom_call" | custom-call | tf_op jit(solution)/shard_map/pallas_call | solution.py:495
  50.2 1.7 %shard_map.95 = (bf16[192,6144]{1,0:T(8,128)(2,1)}, f32[1,192]{1,0:T(1,128)}, bf16[192,1536]{1,0:T(8,128)(2,1)}) custom-call(bf16[2,4,2,48,1536]{4,3,2,1,0:T(8,128)(2,1)S(1)} %get-tuple-element.11.total_all, bf16[2,48,6144]{2,1,0:T(8,128)(2,1)S(1)} %get-tuple-element.12.low_quant, f32[2,2,2,48,128]{4,3,2,1,0:T(8,128)S(1)} %get-tuple-element.13.stat, ...), custom_call_target="tpu_custom_call" | custom-call | tf_op jit(solution)/shard_map/pallas_call | solution.py:548

commit v4 on v3

--- a/solution.py
+++ b/solution.py
@@ -19,7 +19,7 @@
 def kernel(
     dims,
     pos_hbm, key_hbm, value_hbm, gain_hbm, query_hbm, residual_hbm, weight_hbm,
-    total_all, low_quant, stat, gain_all, order_ref,
+    total_all, ready, stat, gain_all, order_ref,
     kv, pos_own, key_raw, value_raw, query_raw, residual_raw, query, residual, weight,
     attended, part, from_core, pair,
     load_sem, x_send, x_recv, z_send, z_recv, gain_send, gain_recv,
@@ -47,24 +47,6 @@
     def inside(offset):
         return (row + offset >= 0) & (row + offset < line)
 
-    barrier = pltpu.get_barrier_semaphore()
-    pl.semaphore_signal(barrier, inc=1, device_id=(partner, tp), device_id_type=MESH)
-    greetings = n_tp
-    for offset in (1, -1, 3):
-        if abs(offset) < line:
-
-            @pl.when(inside(offset))
-            def _():
-                pl.semaphore_signal(
-                    barrier, inc=1, device_id=(at_row(offset), tp), device_id_type=MESH
-                )
-
-            greetings += jnp.where(inside(-offset), 1, 0)
-    for step in range(1, n_tp):
-        pl.semaphore_signal(
-            barrier, inc=1, device_id=(me, lax.rem(tp + step, n_tp)), device_id_type=MESH
-        )
-
     loads = [
         pltpu.make_async_copy(source, target, load_sem.at[index])
         for index, (source, target) in enumerate(
@@ -79,7 +61,28 @@
             )
         )
     ]
-    for load in loads:
+    for load in loads[:3]:
+        load.start()
+
+    barrier = pltpu.get_barrier_semaphore()
+    pl.semaphore_signal(barrier, inc=1, device_id=(partner, tp), device_id_type=MESH)
+    greetings = n_tp
+    for offset in (1, -1, 3):
+        if abs(offset) < line:
+
+            @pl.when(inside(offset))
+            def _():
+                pl.semaphore_signal(
+                    barrier, inc=1, device_id=(at_row(offset), tp), device_id_type=MESH
+                )
+
+            greetings += jnp.where(inside(-offset), 1, 0)
+    for step in range(1, n_tp):
+        pl.semaphore_signal(
+            barrier, inc=1, device_id=(me, lax.rem(tp + step, n_tp)), device_id_type=MESH
+        )
+
+    for load in loads[3:]:
         load.start()
     loads[0].wait()
     first = pos_own[0:1, 0:1]
@@ -88,7 +91,7 @@
     tile_row = lax.broadcasted_iota(jnp.int32, (16, HEAD), 0)
     start = jnp.where(tile_row < 2, jnp.minimum(first, second), jnp.maximum(first, second))
     digit = jnp.where((tile_row & 1) == 0, start >> 6, start & 63)
-    kv[0, row, column, 0, 2 * half :] = digit.astype(F32).astype(BF16)
+    kv[0, row, column, 0, kv_count * half :] = digit.astype(F32).astype(BF16)
     order_ref[...] = jnp.broadcast_to(keep, order_ref.shape)
 
     def split(ref):
@@ -98,15 +101,15 @@
         high = bottom * keep + top * (1.0 - keep)
         return low.astype(BF16), high.astype(BF16)
 
-    for index, ref in enumerate((key_raw, value_raw)):
-        loads[1 + index].wait()
-        low, high = split(ref)
-        for head in range(kv_count):
-            columns = slice(head * HEAD, (head + 1) * HEAD)
-            kind = slice(index * half, (index + 1) * half)
-            kv[0, row, column, head, kind] = low[:, columns]
-            kv[1, row, column, head, kind] = high[:, columns]
-    loads[3].wait()
+    def place(kind, ref):
+        loads[1 + kind].wait()
+        for phase, rows in enumerate(split(ref)):
+            for head in range(kv_count):
+                kv[phase, row, column, kind, head * half : (head + 1) * half] = rows[
+                    :, head * HEAD : (head + 1) * HEAD
+                ]
+
+    place(0, key_raw)
     pl.semaphore_wait(barrier, greetings)
 
 
@@ -132,63 +135,61 @@
             device_id=(partner, tp), device_id_type=MESH,
         ).wait_send()
 
-    def span(phase, head):
-        return slice(0, 2 * half + 16 * (phase == 0 and head == 0))
-
-    def block(phase, source, head):
-        return kv.at[phase, source // 2, lax.rem(source, 2), head, span(phase, head)]
-
-    def along(phase, source, head, offset, when):
+    def span(phase, kind):
+        return slice(0, kv_count * half + 16 * (phase == 0 and kind == 0))
+
+    def block(phase, source, kind):
+        return kv.at[phase, source // 2, lax.rem(source, 2), kind, span(phase, kind)]
+
+    def along(phase, source, kind, offset, when):
         side = 0 if offset > 0 else 1
         target = (at_row(offset), tp)
         remote(
-            block(phase, source, head), block(phase, source, head),
-            z_send.at[phase, head, side], z_recv.at[phase, source // 2, head], target, when,
-        )
-
-    def across(phase, source, head, when=None):
+            block(phase, source, kind), block(phase, source, kind),
+            z_send.at[phase, kind, side], z_recv.at[phase, source // 2, kind], target, when,
+        )
+
+    def across(phase, source, kind, when=None):
         remote(
-            block(phase, source, head), block(phase, source, head),
-            x_send.at[phase, head], x_recv.at[phase, head], (partner, tp), when,
-        )
-
-    def send_own(phase):
-        for head in range(kv_count):
-            across(phase, me, head)
-            for offset in (-1, -3, 1) if phase == 0 else (-1, 1, -3, 3):
-                if abs(offset) < line:
-                    along(phase, me, head, offset, inside(offset))
+            block(phase, source, kind), block(phase, source, kind),
+            x_send.at[phase, kind], x_recv.at[phase, kind], (partner, tp), when,
+        )
+
+    def send_own(phase, kind):
+        across(phase, me, kind)
+        for offset in (-1, -3, 1) if phase == 0 else (-1, 1, -3, 3):
+            if abs(offset) < line:
+                along(phase, me, kind, offset, inside(offset))
 
     def relay(phase, side, distance):
         source = at_row(side * distance)
         there = inside(side * distance)
-        for head in range(kv_count):
+        for kind in range(2):
 
             @pl.when(there)
             def _():
-                landed(block(phase, source, head), z_recv.at[phase, source // 2, head])
+                landed(block(phase, source, kind), z_recv.at[phase, source // 2, kind])
 
             if distance != 2 or (phase == 0 and side < 0):
-                along(phase, source, head, -side, there & inside(-side))
-            across(phase, source, head, there)
+                along(phase, source, kind, -side, there & inside(-side))
+            across(phase, source, kind, there)
 
     relays = [(-1, d) for d in range(1, line)]
     relays += [(1, d) for d in (1, 3, 2) if d < line] + [(1, d) for d in range(4, line)]
 
-    def arrivals(phase):
-        for head in range(kv_count):
-            landed(kv.at[phase, :, 0, head, span(phase, head)], x_recv.at[phase, head])
+    def arrivals(phase, kind):
+        landed(kv.at[phase, :, 0, kind, span(phase, kind)], x_recv.at[phase, kind])
 
     def left_all(phase):
-        for head in range(kv_count):
-            left(kv.at[phase, :, 0, head, span(phase, head)], x_send.at[phase, head])
+        for kind in range(2):
+            left(kv.at[phase, :, 0, kind, span(phase, kind)], x_send.at[phase, kind])
         for index in range(line):
-            ahead = line - 1 - index
+            akind = line - 1 - index
             counts = (
-                1 + (phase == 1 and ahead >= 3) + index - (phase == 1 and index >= 2)
-                if ahead
+                1 + (phase == 1 and akind >= 3) + index - (phase == 1 and index >= 2)
+                if akind
                 else 0,
-                1 + (index >= 3) + ahead - (ahead >= 2) if index else 0,
+                1 + (index >= 3) + akind - (akind >= 2) if index else 0,
             )
 
             @pl.when(row == index)
@@ -196,13 +197,16 @@
                 for side, count in enumerate(counts):
                     if count == 0:
                         continue
-                    for head in range(kv_count):
+                    for kind in range(2):
                         left(
-                            kv.at[phase, 0:count, 0, head, span(phase, head)],
-                            z_send.at[phase, head, side],
+                            kv.at[phase, 0:count, 0, kind, span(phase, kind)],
+                            z_send.at[phase, kind, side],
                         )
 
-    send_own(0)
+    send_own(0, 0)
+    place(1, value_raw)
+    send_own(0, 1)
+    loads[3].wait()
     for step in range(1, n_tp):
         remote(
             gain_all.at[tp], gain_all.at[tp], gain_send.at[0], gain_recv.at[0],
@@ -214,7 +218,8 @@
     residual[0], residual[1] = split(residual_raw)
     for side, distance in relays:
         relay(0, side, distance)
-    send_own(1)
+    for kind in range(2):
+        send_own(1, kind)
 
     rows = lax.broadcasted_iota(jnp.int32, (half, 1), 0).astype(F32)
 
@@ -222,7 +227,7 @@
         lanes = lax.broadcasted_iota(jnp.int32, (1, len(sources) * half), 1)
 
         def base(index):
-            digits = kv[0, index // 2, lax.rem(index, 2), 0, 2 * half :].astype(F32)
+            digits = kv[0, index // 2, lax.rem(index, 2), 0, kv_count * half :].astype(F32)
             return digits[2 * phase : 2 * phase + 1, 0:1] * 64.0 + digits[
                 2 * phase + 1 : 2 * phase + 2, 0:1
             ]
@@ -250,40 +255,57 @@
         ).reshape(stack, half, count)
         return value if mask is None else value + mask[None]
 
-    def weigh(value, peak, value_rows):
+    def weigh(value, peak):
         weights = jnp.exp2((value - peak) * slope)
-        mixed = jnp.dot(
-            weights.astype(BF16).reshape(stack * half, value.shape[2]), value_rows,
+        return jnp.sum(weights, axis=2, keepdims=True), weights.astype(BF16)
+
+    def mix(weights, value_rows):
+        return jnp.dot(
+            weights.reshape(stack * half, weights.shape[2]), value_rows,
             preferred_element_type=F32,
         ).reshape(stack, half, HEAD)
-        return jnp.sum(weights, axis=2, keepdims=True), mixed
+
+    def head_rows(phase, place, kind, kv_head):
+        span_of = slice(kv_head * half, (kv_head + 1) * half)
+        if place is None:
+            return kv[phase, :, :, kind, span_of].reshape(keys, HEAD)
+        return kv[phase, :, place, kind, span_of].reshape(line * half, HEAD)
 
     def put(phase, head, mixed):
         for i in range(stack):
             attended[phase, :, (head + i) * HEAD : (head + i + 1) * HEAD] = mixed[i].astype(BF16)
 
-    def attend_column(side, before):
-        place = column if side == 0 else 1 - column
+    def column_scores(place):
         mask = bias(0, [2 * index + place for index in range(line)])
+        values = []
+        for head in heads:
+            value = scores_of(
+                queries_of(0, head), head_rows(0, place, 0, head // group), mask
+            )
+            values.append((value, jnp.max(value, axis=2, keepdims=True)))
+        return values
+
+    def attend_near():
         results = []
-        for index, head in enumerate(heads):
-            key_rows, value_rows = (
-                kv[0, :, place, head // group, kind * half : (kind + 1) * half].reshape(
-                    line * half, HEAD
-                )
-                for kind in range(2)
-            )
-            value = scores_of(queries_of(0, head), key_rows, mask)
-            peak = jnp.max(value, axis=2, keepdims=True)
-            if side == 0:
-                results.append((peak, *weigh(value, peak, value_rows)))
-                continue
-            old_peak, old_total, old_mixed = before[index]
+        for head, (value, peak) in zip(heads, column_scores(column)):
+            total, weights = weigh(value, peak)
+            results.append((peak, total, mix(weights, head_rows(0, column, 1, head // group))))
+        return results
+
+    def weigh_far(near):
+        results = []
+        for (old_peak, old_total, _), (value, peak) in zip(near, column_scores(1 - column)):
             peak = jnp.maximum(peak, old_peak)
-            total, mixed = weigh(value, peak, value_rows)
+            total, weights = weigh(value, peak)
             shrink = jnp.exp2((old_peak - peak) * slope)
-            put(0, head, (mixed + old_mixed * shrink) / (total + old_total * shrink))
+            inverse = 1.0 / (total + old_total * shrink)
+            results.append((weights, inverse, shrink * inverse))
         return results
+
+    def attend_far(near, far):
+        for head, (_, _, old_mixed), (weights, inverse, shrink) in zip(heads, near, far):
+            mixed = mix(weights, head_rows(0, 1 - column, 1, head // group))
+            put(0, head, mixed * inverse + old_mixed * shrink)
 
     def attend(phase):
         mask = bias(phase, list(range(n_seq)))
@@ -292,7 +314,7 @@
             block_rows = queries_of(phase, head)
             scores = [
                 scores_of(
-                    block_rows, kv[piece, :, :, kv_head, :half].reshape(keys, HEAD),
+                    block_rows, head_rows(piece, None, 0, kv_head),
                     mask if piece == phase else None,
                 )
                 for piece in range(phase + 1)
@@ -303,11 +325,9 @@
             mixed = jnp.zeros((stack, half, HEAD), F32)
             total = jnp.zeros((stack, half, 1), F32)
             for piece, value in enumerate(scores):
-                more, added = weigh(
-                    value, peak, kv[piece, :, :, kv_head, half : 2 * half].reshape(keys, HEAD)
-                )
+                more, weights = weigh(value, peak)
                 total += more
-                mixed += added
+                mixed += mix(weights, head_rows(piece, None, 1, kv_head))
             put(phase, head, mixed / total)
 
     def reduce_tile(phase, index):
@@ -383,17 +403,18 @@
         landed(total_all.at[phase, :, 1 - core], out_recv.at[phase])
         landed(stat.at[phase, 1 - core], stat_recv.at[phase])
 
-    def normalize(phase):
+    def normalize(phase, owner, slot):
+        factor = stat[phase, owner, 1][:, 0:1]
         for part_of in range(n_tp):
-            for owner in range(2):
-                value = total_all[phase, part_of, owner].astype(F32) * gain_all[part_of]
-                factor = stat[phase, owner, 1][:, 0:1]
-                columns = slice(part_of * slice_width, (part_of + 1) * slice_width)
-                low_quant[owner, :, columns] = (value * factor).astype(BF16)
-
-    near = attend_column(0, None)
-    arrivals(0)
-    attend_column(1, near)
+            value = total_all[phase, part_of, owner].astype(F32) * gain_all[part_of]
+            columns = slice(part_of * slice_width, (part_of + 1) * slice_width)
+            ready[slot, :, columns] = (value * factor).astype(BF16)
+
+    near = attend_near()
+    arrivals(0, 0)
+    far = weigh_far(near)
+    arrivals(0, 1)
+    attend_far(near, far)
     loads[6].wait()
     later = [d for d in (1, 3, 2) if d < line] + list(range(4, line))
     project(
@@ -404,27 +425,31 @@
             for side in (-1, 1)
         ],
     )
-    arrivals(1)
+    for kind in range(2):
+        arrivals(1, kind)
     attend(1)
     project(1, [])
     landed(gain_all.at[0 : n_tp - 1], gain_recv.at[0])
     finish(0)
     totals_landed(0)
-    normalize(0)
+    for owner in range(2):
+        normalize(0, owner, owner)
     sends_left(0)
     left(gain_all.at[0 : n_tp - 1], gain_send.at[0])
     finish(1)
+    normalize(1, core, 2)
     totals_landed(1)
     sends_left(1)
 
 
 def assemble(
-    dims, total_all, low_quant, stat, gain_all, order_ref, quant_hbm, scale_hbm, stream_hbm,
+    dims, total_all, ready, stat, gain_all, order_ref, quant_hbm, scale_hbm, stream_hbm,
     quant, scale_row, sem,
 ):
     n_tp, own, slice_width = dims
     tp = lax.axis_index("tp")
-    swap = (jnp.max(order_ref[...]) < 0.5).astype(jnp.int32)
+    swap = (order_ref[0, 0] < 0.5).astype(jnp.int32)
+    mine = lax.rem(tp, 2)
 
     def send(src, dst, index):
         pltpu.make_async_copy(src, dst, sem.at[index]).start()
@@ -434,16 +459,17 @@
         return pl.ds(pl.multiple_of((2 * place + core) * own, own), own)
 
     for core in range(2):
-        send(low_quant.at[core], quant_hbm.at[rows(0, core)], 0)
+        send(ready.at[core], quant_hbm.at[rows(0, core)], 0)
+    send(ready.at[2], quant_hbm.at[rows(1, mine)], 0)
+    for core in range(2):
         for phase in range(2):
             send(total_all.at[phase, tp, core], stream_hbm.at[rows(phase, core)], 1)
-    for core in range(2):
-        factor = stat[1, core, 1][:, 0:1]
-        for part in range(n_tp):
-            columns = slice(part * slice_width, (part + 1) * slice_width)
-            value = total_all[1, part, core].astype(F32) * gain_all[part]
-            quant[core, :, columns] = (value * factor).astype(BF16)
-            send(quant.at[core, :, columns], quant_hbm.at[rows(1, core), columns], 0)
+    factor = stat[1, 1 - mine, 1][:, 0:1]
+    for part in range(n_tp):
+        columns = slice(part * slice_width, (part + 1) * slice_width)
+        value = total_all[1, part, 1 - mine].astype(F32) * gain_all[part]
+        quant[:, columns] = (value * factor).astype(BF16)
+        send(quant.at[:, columns], quant_hbm.at[rows(1, 1 - mine), columns], 0)
     scale = jnp.concatenate(
         [stat[swap if top == 0 else 1 - swap, core, 0] for top in range(2) for core in range(2)],
         axis=0,
@@ -496,7 +522,7 @@
         functools.partial(kernel, (n_seq, n_tp, group, kv_count, half, tiles)),
         out_shape=(
             pltpu.VMEM((2, n_tp, 2, own, slice_width), BF16),
-            pltpu.VMEM((2, own, model), BF16),
+            pltpu.VMEM((3, own, model), BF16),
             pltpu.VMEM((2, 2, 2, own, 128), F32),
             pltpu.VMEM((n_tp, 1, slice_width), F32),
             pltpu.VMEM((8, 128), F32),
@@ -504,7 +530,7 @@
         in_specs=[anywhere] * 7,
         out_specs=(vmem,) * 5,
         scratch_shapes=[
-            pltpu.VMEM((2, line, 2, kv_count, 2 * half + 16, HEAD), BF16),
+            pltpu.VMEM((2, line, 2, 2, kv_count * half + 16, HEAD), BF16),
             pltpu.VMEM((1, token_rows), jnp.int32),
             pltpu.VMEM(key_vectors.shape, BF16),
             pltpu.VMEM(value_vectors.shape, BF16),
@@ -518,10 +544,10 @@
             pltpu.VMEM((2, own, model), BF16),
             pltpu.VMEM((2, n_y, own, model), BF16),
             dma((7,)),
-            dma((2, kv_count)),
-            dma((2, kv_count)),
-            dma((2, kv_count, 2)),
-            dma((2, line, kv_count)),
+            dma((2, 2)),
+            dma((2, 2)),
+            dma((2, 2, 2)),
+            dma((2, line, 2)),
             dma((1,)),
             dma((1,)),
             dma((2,)),
@@ -555,7 +581,7 @@
         in_specs=[vmem] * 5,
         out_specs=(anywhere,) * 3,
         scratch_shapes=[
-            pltpu.VMEM((2, own, model), BF16),
+            pltpu.VMEM((own, model), BF16),
             pltpu.VMEM((1, token_rows), F32),
             dma((3,)),
         ],

time: 52.1 us -> 51.7 us (level)
  Pallas kernels: 51.3 us -> 50.7 us
where the time goes in v4:
time: 51.7 us; the launch traced here: 51.5 us
  Pallas kernels  50.7 us (98%)
  between operations  0.8 us (2%)
    pallas_call x1, Pallas kernels, on_device(): pl.pallas_call(functools.partial(kernel, (n_seq, n_tp, group, kv_count, h...  49.1 us
    pallas_call x1, Pallas kernels, on_device(): pl.pallas_call(functools.partial(assemble, (n_tp, own, slice_width)), out...  1.65 us

profile of v4, /device:TPU:0, one launch (start us, length us, event | category | flops | bytes accessed | tf_op | source)
XLA Modules:
  0.0 51.5 jit_solution(11290683768894082445)
XLA Ops:
  0.6 49.1 %shard_map.94 = (bf16[2,4,2,48,1536]{4,3,2,1,0:T(8,128)(2,1)S(1)}, bf16[3,48,6144]{2,1,0:T(8,128)(2,1)S(1)}, f32[2,2,2,48,128]{4,3,2,1,0:T(8,128)S(1)}, f32[4,1,1536]{2,1,0:T(1,128)S(1)}, f32[8,128]{1,0:T(8,128)S(1)}) custom-call(s32[1,192]{1,0:T(1,128)} %bitcast.2, bf16[192,256]{1,0:T(8,128)(2,1)} %key_hbm.1, bf16[192,256]{1,0:T(8,128)(2,1)} %value_hbm.1, ...), custom_call_target="tpu_custom_call" | custom-call | tf_op jit(solution)/shard_map/pallas_call | solution.py:521
  49.7 1.7 %shard_map.95 = (bf16[192,6144]{1,0:T(8,128)(2,1)}, f32[1,192]{1,0:T(1,128)}, bf16[192,1536]{1,0:T(8,128)(2,1)}) custom-call(bf16[2,4,2,48,1536]{4,3,2,1,0:T(8,128)(2,1)S(1)} %get-tuple-element.11.total_all, bf16[3,48,6144]{2,1,0:T(8,128)(2,1)S(1)} %get-tuple-element.12.ready, f32[2,2,2,48,128]{4,3,2,1,0:T(8,128)S(1)} %get-tuple-element.13.stat, ...), custom_call_target="tpu_custom_call" | custom-call | tf_op jit(solution)/shard_map/pallas_call | solution.py:574

commit v5 on v4

--- a/solution.py
+++ b/solution.py
@@ -135,77 +135,75 @@
             device_id=(partner, tp), device_id_type=MESH,
         ).wait_send()
 
-    def span(phase, kind):
-        return slice(0, kv_count * half + 16 * (phase == 0 and kind == 0))
-
-    def block(phase, source, kind):
-        return kv.at[phase, source // 2, lax.rem(source, 2), kind, span(phase, kind)]
-
-    def along(phase, source, kind, offset, when):
-        side = 0 if offset > 0 else 1
-        target = (at_row(offset), tp)
+    def pieces_of(rows, place, kind):
+        if kind < 2:
+            return kv.at[0, rows, place, kind, 0 : kv_count * half + 16 * (1 - kind)]
+        return kv.at[1, rows, place, :, 0 : kv_count * half]
+
+    def block(source, kind):
+        return pieces_of(source // 2, lax.rem(source, 2), kind)
+
+    def along(source, kind, offset, when):
         remote(
-            block(phase, source, kind), block(phase, source, kind),
-            z_send.at[phase, kind, side], z_recv.at[phase, source // 2, kind], target, when,
-        )
-
-    def across(phase, source, kind, when=None):
+            block(source, kind), block(source, kind),
+            z_send.at[kind, 0 if offset > 0 else 1], z_recv.at[kind, source // 2],
+            (at_row(offset), tp), when,
+        )
+
+    def across(source, kind, when=None):
         remote(
-            block(phase, source, kind), block(phase, source, kind),
-            x_send.at[phase, kind], x_recv.at[phase, kind], (partner, tp), when,
-        )
-
-    def send_own(phase, kind):
-        across(phase, me, kind)
-        for offset in (-1, -3, 1) if phase == 0 else (-1, 1, -3, 3):
+            block(source, kind), block(source, kind), x_send.at[kind], x_recv.at[kind],
+            (partner, tp), when,
+        )
+
+    def send_own(kind):
+        across(me, kind)
+        for offset in (-1, -3, 1) if kind < 2 else (-1, 1, -3, 3):
             if abs(offset) < line:
-                along(phase, me, kind, offset, inside(offset))
-
-    def relay(phase, side, distance):
+                along(me, kind, offset, inside(offset))
+
+    def relay(kinds, side, distance):
         source = at_row(side * distance)
         there = inside(side * distance)
-        for kind in range(2):
+        for kind in kinds:
 
             @pl.when(there)
             def _():
-                landed(block(phase, source, kind), z_recv.at[phase, source // 2, kind])
-
-            if distance != 2 or (phase == 0 and side < 0):
-                along(phase, source, kind, -side, there & inside(-side))
-            across(phase, source, kind, there)
+                landed(block(source, kind), z_recv.at[kind, source // 2])
+
+            if distance != 2 or (kind < 2 and side < 0):
+                along(source, kind, -side, there & inside(-side))
+            across(source, kind, there)
 
     relays = [(-1, d) for d in range(1, line)]
     relays += [(1, d) for d in (1, 3, 2) if d < line] + [(1, d) for d in range(4, line)]
 
-    def arrivals(phase, kind):
-        landed(kv.at[phase, :, 0, kind, span(phase, kind)], x_recv.at[phase, kind])
-
-    def left_all(phase):
-        for kind in range(2):
-            left(kv.at[phase, :, 0, kind, span(phase, kind)], x_send.at[phase, kind])
+    def arrivals(kind):
+        landed(pieces_of(slice(0, line), 0, kind), x_recv.at[kind])
+
+    def left_all():
+        for kind in range(3):
+            left(pieces_of(slice(0, line), 0, kind), x_send.at[kind])
         for index in range(line):
-            akind = line - 1 - index
-            counts = (
-                1 + (phase == 1 and akind >= 3) + index - (phase == 1 and index >= 2)
-                if akind
-                else 0,
-                1 + (index >= 3) + akind - (akind >= 2) if index else 0,
-            )
+            ahead = line - 1 - index
 
             @pl.when(row == index)
             def _():
-                for side, count in enumerate(counts):
-                    if count == 0:
-                        continue
-                    for kind in range(2):
-                        left(
-                            kv.at[phase, 0:count, 0, kind, span(phase, kind)],
-                            z_send.at[phase, kind, side],
-                        )
-
-    send_own(0, 0)
+                for kind in range(3):
+                    direct = kind == 2
+                    counts = (
+                        1 + (direct and ahead >= 3) + index - (direct and index >= 2)
+                        if ahead
+                        else 0,
+                        1 + (index >= 3) + ahead - (ahead >= 2) if index else 0,
+                    )
+                    for side, count in enumerate(counts):
+                        if count:
+                            left(pieces_of(slice(0, count), 0, kind), z_send.at[kind, side])
+
+    send_own(0)
     place(1, value_raw)
-    send_own(0, 1)
+    send_own(1)
     loads[3].wait()
     for step in range(1, n_tp):
         remote(
@@ -217,9 +215,8 @@
     query[0], query[1] = split(query_raw)
     residual[0], residual[1] = split(residual_raw)
     for side, distance in relays:
-        relay(0, side, distance)
-    for kind in range(2):
-        send_own(1, kind)
+        relay((0, 1), side, distance)
+    send_own(2)
 
     rows = lax.broadcasted_iota(jnp.int32, (half, 1), 0).astype(F32)
 
@@ -330,6 +327,11 @@
                 mixed += mix(weights, head_rows(piece, None, 1, kv_head))
             put(phase, head, mixed / total)
 
+    starts = group_starts(len(tiles))
+
+    def slot_of(phase, index):
+        return 0 if phase == 0 else sum(1 for start in starts if start <= index)
+
     def reduce_tile(phase, index):
         columns = tiles[index][2]
         landed(from_core.at[phase, :, columns], core_recv.at[phase, index])
@@ -339,7 +341,7 @@
             target = lax.rem(y + step, n_y) * 2 + core
             remote(
                 pair.at[phase, y, :, columns], pair.at[phase, y, :, columns],
-                y_send.at[phase, step - 1], y_recv.at[phase, n_y - 1 - step, index], (me, target),
+                y_send.at[phase, step - 1], y_recv.at[n_y - 1 - step, slot_of(phase, index)], (me, target),
             )
 
     def project(phase, between):
@@ -370,9 +372,16 @@
         square = jnp.zeros((own, 1), F32)
         peak = jnp.zeros((own, 1), F32)
         for index, (part_of, inner, columns) in enumerate(tiles):
-            for step in range(1, n_y):
-                source = lax.rem(y + step, n_y)
-                landed(pair.at[phase, source, :, columns], y_recv.at[phase, step - 1, index])
+            groups = starts if phase else [0]
+            if index in groups:
+                end = min([start for start in groups if start > index] + [len(tiles)]) - 1
+                wanted = slice(columns.start, tiles[end][2].stop)
+                for step in range(1, n_y):
+                    source = lax.rem(y + step, n_y)
+                    landed(
+                        pair.at[phase, source, :, wanted],
+                        y_recv.at[step - 1, slot_of(phase, index)],
+                    )
             total = pair[phase, 0, :, columns].astype(F32)
             for source in range(1, n_y):
                 total += pair[phase, source, :, columns].astype(F32)
@@ -392,8 +401,6 @@
         )
 
     def sends_left(phase):
-        left_all(phase)
-        left(part.at[phase, 1 - core], core_send.at[phase])
         for step in range(1, n_y):
             left(pair.at[phase, y], y_send.at[phase, step - 1])
         left(total_all.at[phase, :, core], out_send.at[phase])
@@ -411,22 +418,21 @@
             ready[slot, :, columns] = (value * factor).astype(BF16)
 
     near = attend_near()
-    arrivals(0, 0)
+    arrivals(0)
     far = weigh_far(near)
-    arrivals(0, 1)
+    arrivals(1)
     attend_far(near, far)
     loads[6].wait()
     later = [d for d in (1, 3, 2) if d < line] + list(range(4, line))
     project(
         0,
         [
-            (1 + 2 * i, functools.partial(relay, 1, side, distance))
+            (1 + 2 * i, functools.partial(relay, (2,), side, distance))
             for i, distance in enumerate(later)
             for side in (-1, 1)
         ],
     )
-    for kind in range(2):
-        arrivals(1, kind)
+    arrivals(2)
     attend(1)
     project(1, [])
     landed(gain_all.at[0 : n_tp - 1], gain_recv.at[0])
@@ -435,6 +441,9 @@
     for owner in range(2):
         normalize(0, owner, owner)
     sends_left(0)
+    left_all()
+    for phase in range(2):
+        left(part.at[phase, 1 - core], core_send.at[phase])
     left(gain_all.at[0 : n_tp - 1], gain_send.at[0])
     finish(1)
     normalize(1, core, 2)
@@ -454,13 +463,22 @@
     def send(src, dst, index):
         pltpu.make_async_copy(src, dst, sem.at[index]).start()
 
-    def rows(phase, core):
+    def rows(phase, core, first=0, count=own):
         place = swap if phase == 0 else 1 - swap
-        return pl.ds(pl.multiple_of((2 * place + core) * own, own), own)
+        start = pl.multiple_of((2 * place + core) * own, own) + first
+        return pl.ds(pl.multiple_of(start, count), count)
+
+    def send_rows(slot, phase, core):
+        count = math.gcd(own, 16)
+        for first in range(0, own, count):
+            send(
+                ready.at[slot, first : first + count],
+                quant_hbm.at[rows(phase, core, first, count)], 0,
+            )
 
     for core in range(2):
-        send(ready.at[core], quant_hbm.at[rows(0, core)], 0)
-    send(ready.at[2], quant_hbm.at[rows(1, mine)], 0)
+        send_rows(core, 0, core)
+    send_rows(2, 1, mine)
     for core in range(2):
         for phase in range(2):
             send(total_all.at[phase, tp, core], stream_hbm.at[rows(phase, core)], 1)
@@ -484,6 +502,12 @@
     send(scale_row, scale_hbm, 2)
     for index, array in enumerate((quant_hbm, stream_hbm, scale_hbm)):
         pltpu.make_async_copy(array, array, sem.at[index]).wait()
+
+
+def group_starts(count):
+    if count < 6:
+        return list(range(count))
+    return [0] + list(range(4, count - 2, 2)) + [count - 2, count - 1]
 
 
 def tiles_of(n_tp, slice_width):
@@ -544,16 +568,16 @@
             pltpu.VMEM((2, own, model), BF16),
             pltpu.VMEM((2, n_y, own, model), BF16),
             dma((7,)),
-            dma((2, 2)),
-            dma((2, 2)),
-            dma((2, 2, 2)),
-            dma((2, line, 2)),
+            dma((3,)),
+            dma((3,)),
+            dma((3, 2)),
+            dma((3, line)),
             dma((1,)),
             dma((1,)),
             dma((2,)),
             dma((2, count)),
             dma((2, n_y - 1)),
-            dma((2, n_y - 1, count)),
+            dma((n_y - 1, 1 + len(group_starts(count)))),
             dma((2,)),
             dma((2,)),
             dma((2,)),

time: 51.7 us -> 51.3 us (level)
  no operation moved by 1% of the time
where the time goes in v5:
time: 51.3 us; the launch traced here: 51.2 us
  Pallas kernels  50.5 us (98%)
  between operations  0.64 us (1%)
    pallas_call x1, Pallas kernels, on_device(): pl.pallas_call(functools.partial(kernel, (n_seq, n_tp, group, kv_count, h...  48.9 us
    pallas_call x1, Pallas kernels, on_device(): pl.pallas_call(functools.partial(assemble, (n_tp, own, slice_width)), out...  1.65 us

profile of v5, /device:TPU:0, one launch (start us, length us, event | category | flops | bytes accessed | tf_op | source)
XLA Modules:
  0.0 51.2 jit_solution(10534938039258221506)
XLA Ops:
  0.6 48.9 %shard_map.94 = (bf16[2,4,2,48,1536]{4,3,2,1,0:T(8,128)(2,1)S(1)}, bf16[3,48,6144]{2,1,0:T(8,128)(2,1)S(1)}, f32[2,2,2,48,128]{4,3,2,1,0:T(8,128)S(1)}, f32[4,1,1536]{2,1,0:T(1,128)S(1)}, f32[8,128]{1,0:T(8,128)S(1)}) custom-call(s32[1,192]{1,0:T(1,128)} %bitcast.2, bf16[192,256]{1,0:T(8,128)(2,1)} %key_hbm.1, bf16[192,256]{1,0:T(8,128)(2,1)} %value_hbm.1, ...), custom_call_target="tpu_custom_call" | custom-call | tf_op jit(solution)/shard_map/pallas_call | solution.py:545
  49.5 1.7 %shard_map.95 = (bf16[192,6144]{1,0:T(8,128)(2,1)}, f32[1,192]{1,0:T(1,128)}, bf16[192,1536]{1,0:T(8,128)(2,1)}) custom-call(bf16[2,4,2,48,1536]{4,3,2,1,0:T(8,128)(2,1)S(1)} %get-tuple-element.11.total_all, bf16[3,48,6144]{2,1,0:T(8,128)(2,1)S(1)} %get-tuple-element.12.ready, f32[2,2,2,48,128]{4,3,2,1,0:T(8,128)S(1)} %get-tuple-element.13.stat, ...), custom_call_target="tpu_custom_call" | custom-call | tf_op jit(solution)/shard_map/pallas_call | solution.py:598
